TPU v7x, 32 devices: a whole 2x2x4 slice. The times are simulated.
32 devices in a mesh: scan: 4 (over y, core), ascan: 8 (over z, x).
Axes of the slice: x: 2, y: 2, z: 4, core: 2. Of those that a mesh axis runs over, the one named last changes fastest.
Arguments:
- spectra: bfloat16 [8, 4, 1024, 2048], P('scan', None, 'ascan'), may hold values from -8 to 8
- surface_top: int32 [8, 1024], P('scan', 'ascan'), may hold values from 0 to 3, as said below
- surface_bottom: int32 [8, 1024], P('scan', 'ascan'), may hold values from 1 to 8, as said below
Outputs:
- angiogram: float32 [8, 1024, 1024], P('scan', 'ascan')
- structure_map: float32 [8, 1024, 1024], P('scan', 'ascan')
- speckle_map: float32 [8, 1024, 1024], P('scan', 'ascan')
- mean_flow: float32 [], replicated
Inputs may be any that keep to these rules, and one draw needn't show every extreme that they name: surface_top counts tiles of 128 depth rows. surface_bottom is greater than surface_top of the same A-scan.
All inputs are finite; a program needn't handle non-finite values.
Results may differ from a plain program's by a relative error of at most 0.0032.
Values sent between devices are 32-bit elements; how exact they have to be, the bound alone decides.
No kernel may reach another device: no remote copies, remote signals or barrier semaphores. Data moves between devices by JAX's collectives and lax.ppermute only.
A program may use at most 128 MiB of HBM per device.

v0:
```python
import functools
import math

import jax
import jax.numpy as jnp
import numpy as np
from jax import lax
from jax.experimental import pallas as pl
from jax.experimental.pallas import tpu as pltpu
from jax.sharding import PartitionSpec as P


REPEATS = 4
BINS = 2048
BANDS = 4
TILE = 128
BAND_BINS = 512
DEPTH = 1024
TILES = DEPTH // TILE
FLOOR = 0.05 * BAND_BINS
VARIANCE_SCALE = 0.1
HEAD = 2
MAPS = 3


def table_values():
    sample = np.arange(BAND_BINS)
    depth = np.arange(DEPTH)
    product = (sample[:, None] * depth[None, :]) % BINS
    angle = product.astype(np.float32) * np.float32(2.0 * math.pi / BINS)
    window = np.sin(np.float32(math.pi) * (sample.astype(np.float32) + 0.5) / BAND_BINS) ** 2
    return window[:, None] * np.cos(angle), window[:, None] * np.sin(angle)


def tile_tables(width):
    cosine, sine = table_values()
    slabs = DEPTH // width
    cosine = cosine.reshape(BAND_BINS, slabs, width)
    sine = sine.reshape(BAND_BINS, slabs, width)
    both = np.concatenate([cosine, sine], axis=2).transpose(1, 0, 2)
    return jnp.asarray(both.astype(np.float32)).astype(jnp.bfloat16)


def moments_rows(profile_ref, buf, out_ref, slot, scan, ascans, begin, end):
    tiny = jnp.float32(np.finfo(np.float32).tiny)
    step = 8
    for start in range(begin, end, step):
        sim = amp = var1 = var2 = None
        for band in range(BANDS):
            power, amplitude = [], []
            for repeat in range(REPEATS):
                base = repeat * ascans + start
                re = profile_ref[buf, band, base : base + step, :TILE]
                im = profile_ref[buf, band, base : base + step, TILE:]
                p = re * re + im * im
                power.append(p)
                amplitude.append(p * lax.rsqrt(jnp.maximum(p, tiny)))
            parts = []
            for r in range(REPEATS - 1):
                root = lax.rsqrt(jnp.maximum(power[r] + power[r + 1], FLOOR))
                parts.append((amplitude[r] * root) * (amplitude[r + 1] * root))
            s = parts[0] + parts[1] + parts[2]
            s01 = amplitude[0] + amplitude[1]
            s23 = amplitude[2] + amplitude[3]
            d01 = amplitude[0] - amplitude[1]
            d23 = amplitude[2] - amplitude[3]
            a = s01 + s23
            d = s01 - s23
            v1 = d01 * d01 + d23 * d23
            v2 = d * d
            sim = s if sim is None else sim + s
            amp = a if amp is None else amp + a
            var1 = v1 if var1 is None else var1 + v1
            var2 = v2 if var2 is None else var2 + v2
        rows = pl.ds(scan * ascans + start, step)
        out_ref[slot, rows, 0:TILE] = 1.0 - sim * (2.0 / (BANDS * (REPEATS - 1)))
        out_ref[slot, rows, TILE : 2 * TILE] = amp * (1.0 / (BANDS * REPEATS * math.sqrt(BAND_BINS)))
        out_ref[slot, rows, 2 * TILE :] = (var1 + 0.5 * var2) * (
            0.5 / (REPEATS * BANDS * VARIANCE_SCALE * BAND_BINS)
        )


def split(x):
    high = x.astype(jnp.bfloat16)
    low = (x - high.astype(jnp.float32)).astype(jnp.bfloat16)
    return high, low


def tissue(top, bottom, tile):
    rows = top.shape[1]
    mask = jnp.where((top <= tile) & (tile < bottom), 1.0, 0.0).astype(jnp.float32)
    before = lax.broadcasted_iota(jnp.int32, (rows, rows), 0) < lax.broadcasted_iota(
        jnp.int32, (rows, rows), 1
    )
    spread = jnp.broadcast_to(mask, (8, rows)).astype(jnp.bfloat16)
    rank = jnp.dot(spread, before.astype(jnp.bfloat16), preferred_element_type=jnp.float32)[0:1]
    return mask, jnp.where(mask > 0.0, rank, -1.0).astype(jnp.int32)


def chooser(rank, first, count):
    rows = rank.shape[1]
    index = lax.broadcasted_iota(jnp.int32, (count, rows), 0) + first
    return jnp.where(index == rank, 1.0, 0.0).astype(jnp.bfloat16)


def flat_rows(block):
    return jnp.concatenate([block[i : i + 1] for i in range(block.shape[0])], axis=1)


def peer_target(peer, me, half):
    kind, index = peer
    if kind == "far":
        return ((me & half) ^ half) | ((me + index) & (half - 1))
    return me ^ index if kind == "near" else index


def peer_origin(peer, me, half):
    kind, index = peer
    if kind == "far":
        return ((me & half) ^ half) | ((me + half - index) & (half - 1))
    return me ^ index if kind == "near" else index


def send_kernel(peers, messages, rooms, x_ref, table_ref, top_ref, bottom_ref, stats_in, *refs):
    outs = refs[: sum(len(m) for m in messages)]
    stats_ref, profile_ref, maps_ref = refs[len(outs) :]
    slots = len(peers)
    scans, _, ascans, _ = x_ref.shape
    me = lax.axis_index("ascan")
    half = lax.axis_size("ascan") // 2
    tiles = [jnp.asarray(peer_target(p, me, half), jnp.int32) for p in peers]

    def pick(slot):
        if isinstance(slot, int):
            return tiles[slot]
        chosen = tiles[0]
        for i in range(1, slots):
            chosen = jnp.where(slot == i, tiles[i], chosen)
        return chosen

    def product(weights, scan, buf, band):
        lanes = slice(band * BAND_BINS, (band + 1) * BAND_BINS)
        x = x_ref[scan, :, :, lanes].reshape(REPEATS * ascans, BAND_BINS)
        profile_ref[buf, band] = jnp.dot(x, weights, preferred_element_type=jnp.float32)

    def both(following, current):
        weights = table_ref[pick(following[0])] if following else None
        share = ascans // BANDS
        for band in range(BANDS):
            if following:
                product(weights, following[1], following[1] % 2, band)
            if current:
                moments_rows(
                    profile_ref, current[1] % 2, maps_ref, *current, ascans, band * share, (band + 1) * share
                )

    if slots == 1:
        both((0, 0), None)
        for scan in range(scans - 1):
            both((0, scan + 1), (0, scan))
        both(None, (0, scans - 1))
    else:
        both((0, 0), None)

        def step(slot, carry):
            for scan in range(scans - 1):
                both((slot, scan + 1), (slot, scan))
            both((jnp.minimum(slot + 1, slots - 1), 0), (slot, scans - 1))
            return carry

        lax.fori_loop(0, slots, step, 0)

    top = flat_rows(top_ref[...])
    bottom = flat_rows(bottom_ref[...])
    rows = top.shape[1]
    flow = jnp.zeros((8, TILE), jnp.float32)
    held = over = jnp.float32(0.0)
    position = 0
    for slot, parts in enumerate(messages):
        mask, rank = tissue(top, bottom, tiles[slot])
        high, low = split(maps_ref[slot])
        spread = jnp.broadcast_to(mask, (8, rows)).astype(jnp.bfloat16)
        flow += jnp.dot(spread, high[:, :TILE], preferred_element_type=jnp.float32)
        flow += jnp.dot(spread, low[:, :TILE], preferred_element_type=jnp.float32)
        count = jnp.sum(mask)
        held += count
        room = jnp.float32(rows)
        for source, value in enumerate(rooms[slot]):
            room = jnp.where(me == source, jnp.float32(value), room)
        over = jnp.where(count > room, 1.0, over)
        for first, size, carried, header in parts:
            out = outs[position]
            position += 1
            choice = chooser(rank, first, size)
            out[...] = jnp.dot(choice, high, preferred_element_type=jnp.float32) + jnp.dot(
                choice, low, preferred_element_type=jnp.float32
            )
            if header:
                out[carried : carried + 1, 0:rows] = top.astype(jnp.float32)
                out[carried + 1 : carried + 2, 0:rows] = bottom.astype(jnp.float32)
    line = lax.broadcasted_iota(jnp.int32, (8, TILE), 0)
    stats_ref[...] = stats_in[...] + jnp.where(
        line == 0, flow, jnp.where(line == 1, held, jnp.where(line == 2, over, 0.0))
    )


VMEM = pl.BlockSpec(memory_space=pltpu.VMEM)


def send(peers, spectra, tables, top, bottom, stats, messages, rooms):
    scans, repeats, ascans, bins = spectra.shape
    assert scans % 2 == 0
    rows = scans * ascans
    shapes = [
        jax.ShapeDtypeStruct((size, MAPS * TILE), jnp.float32)
        for parts in messages
        for _, size, _, _ in parts
    ]
    shapes.append(jax.ShapeDtypeStruct((8, TILE), jnp.float32))
    return pl.pallas_call(
        functools.partial(send_kernel, peers, messages, rooms),
        out_shape=shapes,
        in_specs=[VMEM] * 5,
        out_specs=[VMEM] * len(shapes),
        scratch_shapes=[
            pltpu.VMEM((2, BANDS, repeats * ascans, 2 * TILE), jnp.float32),
            pltpu.VMEM((len(peers), rows, MAPS * TILE), jnp.float32),
        ],
        cost_estimate=pl.CostEstimate(
            flops=2 * rows * repeats * bins * 2 * TILE * len(peers),
            bytes_accessed=2 * spectra.size,
            transcendentals=0,
        ),
        compiler_params=pltpu.CompilerParams(vmem_limit_bytes=32 * 1024 * 1024),
    )(spectra, tables, top, bottom, stats)


def receive_kernel(peers, messages, totals_ref, top_ref, bottom_ref, *refs):
    count = sum(len(m) for m in messages)
    ins = refs[:count]
    angiogram_ref, structure_ref, speckle_ref, decorrelation_ref = refs[count:]
    scans = angiogram_ref.shape[0]
    total = angiogram_ref.shape[2]
    own_top = flat_rows(top_ref[...])
    own_bottom = flat_rows(bottom_ref[...])
    rows = own_top.shape[1]
    ascans = rows // scans
    me = lax.axis_index("ascan")
    half = lax.axis_size("ascan") // 2
    position = 0
    for peer, parts in zip(peers, messages):
        pieces = ins[position : position + len(parts)]
        position += len(parts)
        top, bottom = own_top, own_bottom
        for piece, (_, _, carried, header) in zip(pieces, parts):
            if header:
                top = piece[carried : carried + 1, 0:rows].astype(jnp.int32)
                bottom = piece[carried + 1 : carried + 2, 0:rows].astype(jnp.int32)
        _, rank = tissue(top, bottom, me)
        result = None
        for piece, (first, size, carried, header) in zip(pieces, parts):
            choice = chooser(jnp.where(rank < first + carried, rank, -1), first, size)
            for part in split(piece[...]):
                term = lax.dot_general(
                    part, choice, (((0,), (0,)), ((), ())), preferred_element_type=jnp.float32
                )
                result = term if result is None else result + term
        origin = jnp.asarray(peer_origin(peer, me, half), jnp.int32)
        lanes = pl.ds(pl.multiple_of(origin * ascans, ascans), ascans)
        for scan in range(scans):
            columns = slice(scan * ascans, (scan + 1) * ascans)
            decorrelation_ref[scan, :, lanes] = result[0:TILE, columns]
            structure_ref[scan, :, lanes] = result[TILE : 2 * TILE, columns]
            speckle_ref[scan, :, lanes] = result[2 * TILE :, columns]
    flow = jnp.sum(totals_ref[0:1, :], axis=1, keepdims=True)
    scale = (totals_ref[1:2, 0:1] * TILE) / (3.0 * flow)
    step = 8
    for scan in range(scans):
        for start in range(0, TILE, step):
            d = decorrelation_ref[scan, start : start + step, :]
            lane = lax.broadcasted_iota(jnp.int32, d.shape, 1)
            left = jnp.where(lane == 0, 0.0, pltpu.roll(d, 1, 1))
            right = jnp.where(lane == total - 1, 0.0, pltpu.roll(d, total - 1, 1))
            angiogram_ref[scan, start : start + step, :] = ((left + d) + right) * scale


def receive(peers, totals, top, bottom, pieces, messages, members):
    scans, ascans = top.shape
    shape = jax.ShapeDtypeStruct((scans, TILE, members * ascans), jnp.float32)
    return pl.pallas_call(
        functools.partial(receive_kernel, peers, messages),
        out_shape=[shape] * MAPS,
        in_specs=[VMEM] * (3 + len(pieces)),
        out_specs=[VMEM] * MAPS,
        scratch_shapes=[pltpu.VMEM(shape.shape, jnp.float32)],
        cost_estimate=pl.CostEstimate(
            flops=2 * 2 * scans * ascans * 256 * MAPS * TILE * members,
            bytes_accessed=8 * MAPS * scans * TILE * members * ascans,
            transcendentals=0,
        ),
        compiler_params=pltpu.CompilerParams(vmem_limit_bytes=32 * 1024 * 1024),
    )(totals, top, bottom, *pieces)


def capacities(members, scans, ascans):
    total = members * ascans
    position = np.arange(total)
    chance = np.zeros((total, TILES))
    half = TILES // 2
    for top in range(half):
        reach = 1 + (TILES - top - 1) * (position + 1) // total
        for tile in range(top, TILES):
            chance[:, tile] += np.clip(reach - (tile - top), 0, None) / reach / half
    mean = chance.reshape(members, ascans, TILES).sum(1) * scans
    spread = np.sqrt((chance * (1 - chance)).reshape(members, ascans, TILES).sum(1) * scans)
    caps = np.ceil(mean + 3.8 * spread)
    return np.minimum(caps, scans * ascans).astype(int)


def plan_levels(caps, matching, merge):
    need = [int(caps[s, d]) + (HEAD if s != d else 0) for s, d in matching]
    base = sorted(need)[len(need) // 2]
    need = [max(n, base) for n in need]
    marks = []
    for value in sorted(set(-(-n // 8) * 8 for n in need)):
        if len(marks) > 1 and value - marks[-1] < merge:
            marks[-1] = value
        else:
            marks.append(value)
    messages, pair_lists, room, below = [], [], [0] * len(need), 0
    for mark in marks:
        pairs = [pair for pair, n in zip(matching, need) if n > below]
        head = HEAD if below == 0 else 0
        for s, _ in pairs:
            room[s] = mark - HEAD
        first = max(below - HEAD, 0)
        messages.append((first, mark - below, mark - below - head, head > 0))
        pair_lists.append(pairs)
        below = mark
    return tuple(messages), pair_lists, tuple(room)


def exchange_plans(members, scans, ascans):
    rows = scans * ascans
    half = members // 2
    caps = capacities(members, scans, ascans)
    far = [("far", m) for m in range(half)]
    near = [("near", j) for j in range(1, half)]
    own = ("near", 0)

    def pairs_of(peer):
        return [(s, int(peer_target(peer, s, half))) for s in range(members)]

    plans = {peer: plan_levels(caps, pairs_of(peer), 24) for peer in far}
    widest = max(int(caps[s, d]) for peer in near for s, d in pairs_of(peer))
    size = min(-(-(widest + HEAD) // 8) * 8, rows)
    for peer in near:
        plans[peer] = (
            ((0, size, size - HEAD, True),),
            [pairs_of(peer)],
            (size - HEAD,) * members,
        )
    plans[own] = (((0, rows, rows, False),), [None], (rows,) * members)
    return plans, far, near, own


def sparse_body(members, spectra, top, bottom):
    scans, _, ascans, _ = spectra.shape
    rows = scans * ascans
    half = members // 2
    tables = tile_tables(TILE)
    plans, far, near, own = exchange_plans(members, scans, ascans)
    stats = jnp.zeros((8, TILE), jnp.float32)
    sent = {}
    for number, group in enumerate((far[:1], far[1:2], far[2:], near + [own])):
        *out, stats = send(
            group,
            spectra,
            tables,
            top,
            bottom,
            stats,
            [plans[p][0] for p in group],
            [plans[p][2] for p in group],
        )
        for peer in group:
            for level in range(len(plans[peer][0])):
                sent[peer, level] = out.pop(0)
    received = []
    for peer in far + near + [own]:
        for level, pairs in enumerate(plans[peer][1]):
            message = sent[peer, level]
            if pairs is not None:
                message = lax.ppermute(message, "ascan", pairs)
            received.append(message)
    number = 0
    totals = stats
    for axis, length in (("scan", lax.axis_size("scan")), ("ascan", members)):
        stride = 1
        while stride < length:
            totals = totals + lax.ppermute(totals, axis, [(s, s ^ stride) for s in range(length)])
            stride *= 2
            number += 1
    mean_flow = jnp.sum(totals[0]) / (totals[1, 0] * TILE)

    def quick(received):
        peers = far + near + [own]
        messages = [plans[p][0] for p in peers]
        return tuple(receive(peers, totals, top, bottom, received, messages, members))

    def dense(received):
        everyone = [("all", t) for t in range(TILES)]
        message = ((0, rows + 8, rows, True),)
        out = []
        for part in (everyone[:half], everyone[half:]):
            *some, _ = send(
                part, spectra, tables, top, bottom, totals,
                [message] * half, [(rows,) * members] * half,
            )
            out += some
        swapped = lax.all_to_all(jnp.stack(out), "ascan", 0, 0, tiled=True)
        pieces = [swapped[i] for i in range(members)]
        return tuple(receive(everyone, totals, top, bottom, pieces, [message] * members, members))

    outs = lax.cond(totals[2, 0] > 0.0, dense, quick, received)
    return (*outs, mean_flow)


def plain_body(spectra, surface_top, surface_bottom):
    scans, repeats, ascans, _ = spectra.shape
    cosine, sine = table_values()
    table = jnp.asarray(np.concatenate([cosine, sine], axis=1).astype(np.float32)).astype(jnp.bfloat16)
    similarity = amplitude_sum = variance = jnp.zeros((scans, ascans, DEPTH), jnp.float32)
    for band in range(BANDS):
        part = spectra[..., band * BAND_BINS : (band + 1) * BAND_BINS]
        profile = jnp.dot(part.reshape(-1, BAND_BINS), table, preferred_element_type=jnp.float32)
        profile = profile.reshape(scans, repeats, ascans, 2 * DEPTH)
        amplitude = jnp.sqrt(profile[..., :DEPTH] ** 2 + profile[..., DEPTH:] ** 2)
        first, second = amplitude[:, :-1], amplitude[:, 1:]
        similarity += jnp.sum(
            2.0 * first * second / jnp.maximum(first**2 + second**2, FLOOR), axis=1
        )
        amplitude_sum += jnp.sum(amplitude, axis=1)
        center = jnp.mean(amplitude, axis=1, keepdims=True)
        variance += jnp.mean((amplitude - center) ** 2, axis=1)
    depth = jnp.arange(DEPTH, dtype=jnp.int32)
    inside = (depth >= surface_top[..., None] * TILE) & (depth < surface_bottom[..., None] * TILE)
    inside = inside.astype(jnp.float32)
    decorrelation = (1.0 - similarity / (BANDS * (REPEATS - 1))) * inside
    structure = amplitude_sum / (BANDS * REPEATS) / math.sqrt(BAND_BINS) * inside
    speckle = variance / BANDS / (VARIANCE_SCALE * BAND_BINS) * inside
    totals = lax.psum((jnp.sum(decorrelation), jnp.sum(inside)), ("scan", "ascan"))
    mean_flow = totals[0] / totals[1]
    decorrelation, structure, speckle = (
        lax.all_to_all(x, "ascan", split_axis=2, concat_axis=1, tiled=True)
        for x in (decorrelation, structure, speckle)
    )
    padded = jnp.pad(decorrelation, ((0, 0), (1, 1), (0, 0)))
    smoothed = (padded[:, :-2] + padded[:, 1:-1] + padded[:, 2:]) / 3.0
    angiogram = jnp.swapaxes(smoothed / mean_flow, 1, 2)
    return (angiogram, jnp.swapaxes(structure, 1, 2), jnp.swapaxes(speckle, 1, 2), mean_flow)


def solution(mesh):
    members = mesh.shape["ascan"]
    scans = mesh.shape["scan"]

    def fits(spectra):
        local_scans, ascans = spectra.shape[0] // scans, spectra.shape[2] // members
        return (
            members == TILES
            and scans & (scans - 1) == 0
            and local_scans % 2 == 0
            and ascans == TILE
            and local_scans * ascans <= MAPS * TILE
        )

    def program(spectra, surface_top, surface_bottom):
        sparse = fits(spectra)
        body = functools.partial(sparse_body, members) if sparse else plain_body
        step = jax.shard_map(
            body,
            mesh=mesh,
            in_specs=(P("scan", None, "ascan", None), P("scan", "ascan"), P("scan", "ascan")),
            out_specs=(
                P("scan", "ascan", None),
                P("scan", "ascan", None),
                P("scan", "ascan", None),
                P(),
            ),
            check_vma=False,
        )
        return step(spectra, surface_top, surface_bottom)

    return program
```

profile of v0, /device:TPU:0, one launch (start us, length us, event | category | flops | bytes accessed | tf_op | source)
XLA Modules:
  0.0 99.3 jit_solution(491070382960176907)
XLA Ops:
  0.6 0.0 copy-start.2
  0.6 0.0 copy-start.4
  0.7 0.0 copy-start.3
  0.7 0.0 copy-start
  0.7 5.2 %shard_map.75 = (f32[96,384]{1,0:T(8,128)S(1)}, f32[56,384]{1,0:T(8,128)S(1)}, f32[40,384]{1,0:T(8,128)S(1)}, f32[32,384]{1,0:T(8,128)S(1)}, f32[8,128]{1,0:T(8,128)S(1)}) custom-call(bf16[2,4,128,2048]{3,2,1,0:T(8,128)(2,1)} %x_ref.8, bf16[8,512,256]{2,1,0:T(8,128)(2,1)} %constant.14.table_ref, s32[2,128]{1,0:T(2,128)} %top_ref.8, s32[2,128]{1,0:T(2,128)} %bottom_ref.8, ...), custom_call_target="tpu_custom_call" | custom-call | flops 1073741824 | bytes 4194304 | tf_op jit(solution)/shard_map/pallas_call | solution.py:220
  5.9 0.7 collective-permute-start.8
  6.6 2.2 %shard_map.76 = (f32[96,384]{1,0:T(8,128)S(1)}, f32[56,384]{1,0:T(8,128)S(1)}, f32[40,384]{1,0:T(8,128)S(1)}, f32[24,384]{1,0:T(8,128)S(1)}, f32[8,128]{1,0:T(8,128)S(1)}) custom-call(bf16[2,4,128,2048]{3,2,1,0:T(8,128)(2,1)S(1)} %copy-done, bf16[8,512,256]{2,1,0:T(8,128)(2,1)S(1)} %copy-done.2, s32[2,128]{1,0:T(2,128)S(1)} %copy-done.3, ...), custom_call_target="tpu_custom_call" | custom-call | flops 1073741824 | bytes 4194304 | tf_op jit(solution)/shard_map/pallas_call | solution.py:220
  8.8 0.7 collective-permute-start.12
  9.5 5.0 %shard_map.77 = (f32[96,384]{1,0:T(8,128)S(1)}, f32[56,384]{1,0:T(8,128)S(1)}, f32[32,384]{1,0:T(8,128)S(1)}, f32[24,384]{1,0:T(8,128)S(1)}, f32[96,384]{1,0:T(8...) custom-call(bf16[2,4,128,2048]{3,2,1,0:T(8,128)(2,1)S(1)} %copy-done, ...), custom_call_target="tpu_custom_call" | custom-call | flops 2147483648 | bytes 4194304 | tf_op jit(solution)/shard_map/pallas_call | solution.py:220
  14.5 0.7 collective-permute-start.16
  15.2 9.7 %shard_map.78 = (f32[184,384]{1,0:T(8,128)S(1)}, f32[184,384]{1,0:T(8,128)S(1)}, f32[184,384]{1,0:T(8,128)S(1)}, f32[256,384]{1,0:T(8,128)}, f32[8,128]{1,0:T(8,128)S(1)}) custom-call(bf16[2,4,128,2048]{3,2,1,0:T(8,128)(2,1)S(1)} %copy-done, bf16[8,512,256]{2,1,0:T(8,128)(2,1)S(1)} %copy-done.2, s32[2,128]{1,0:T(2,128)S(1)} %copy-done.3, ...), custom_call_target="tpu_custom_call" | custom-call | flops 4294967296 | bytes 4194304 | tf_op jit(solution)/shard_map/pallas_call | solution.py:220
  24.9 0.5 collective-permute-start
  25.4 0.8 collective-permute-done
  26.3 2.9 %collective-permute-start.1 = (f32[8,128]{1,0:T(8,128)S(1)}, f32[8,128]{1,0:T(8,128)S(1)}, u32[]{:S(2)}, u32[]{:S(2)}) collective-permute-start(f32[8,128]{1,0:T(8,128)S(1)} %add.15), channel_id=1, source_target_pairs={{0,16},{8,24},{16,0},{24,8},{1,17},{9,25},{17,1},{25,9},{2,18},{10... | collective-permute-start | bytes 12296 | tf_op jit(solution)/shard_map/ppermute | solution.py:401
  29.1 1.6 %collective-permute-done.1 = f32[8,128]{1,0:T(8,128)S(1)} collective-permute-done((f32[8,128]{1,0:T(8,128)S(1)}, f32[8,128]{1,0:T(8,128)S(1)}, u32[]{:S(2)}, u32[]{:S(2)}) %collective-permute-start.1) | collective-permute-done | bytes 4128 | tf_op jit(solution)/shard_map/ppermute | solution.py:401
  30.7 2.0 %collective-permute-start.2 = (f32[8,128]{1,0:T(8,128)S(1)}, f32[8,128]{1,0:T(8,128)S(1)}, u32[]{:S(2)}, u32[]{:S(2)}) collective-permute-start(f32[8,128]{1,0:T(8,128)S(1)} %add.16), channel_id=1, source_target_pairs={{0,1},{1,0},{2,3},{3,2},{4,5},{5,4},{6,7},{7,6},{8,9},{9,8},{10,11... | collective-permute-start | bytes 12296 | tf_op jit(solution)/shard_map/ppermute | solution.py:401
  32.7 0.7 collective-permute-start.6
  33.4 1.0 collective-permute-done.2
  34.3 3.4 %collective-permute-start.3 = (f32[8,128]{1,0:T(8,128)S(1)}, f32[8,128]{1,0:T(8,128)S(1)}, u32[]{:S(2)}, u32[]{:S(2)}) collective-permute-start(f32[8,128]{1,0:T(8,128)S(1)} %add.17), channel_id=1, source_target_pairs={{0,2},{1,3},{2,0},{3,1},{4,6},{5,7},{6,4},{7,5},{8,10},{9,11},{10,... | collective-permute-start | bytes 12296 | tf_op jit(solution)/shard_map/ppermute | solution.py:401
  37.7 1.6 %collective-permute-done.3 = f32[8,128]{1,0:T(8,128)S(1)} collective-permute-done((f32[8,128]{1,0:T(8,128)S(1)}, f32[8,128]{1,0:T(8,128)S(1)}, u32[]{:S(2)}, u32[]{:S(2)}) %collective-permute-start.3) | collective-permute-done | bytes 4128 | tf_op jit(solution)/shard_map/ppermute | solution.py:401
  39.3 4.4 %collective-permute-start.4 = (f32[8,128]{1,0:T(8,128)S(1)}, f32[8,128]{1,0:T(8,128)S(1)}, u32[]{:S(2)}, u32[]{:S(2)}) collective-permute-start(f32[8,128]{1,0:T(8,128)S(1)} %add.18), channel_id=1, source_target_pairs={{0,4},{1,5},{2,6},{3,7},{4,0},{5,1},{6,2},{7,3},{8,12},{9,13},{10,... | collective-permute-start | bytes 12296 | tf_op jit(solution)/shard_map/ppermute | solution.py:401
  43.7 1.6 %collective-permute-done.4 = f32[8,128]{1,0:T(8,128)S(1)} collective-permute-done((f32[8,128]{1,0:T(8,128)S(1)}, f32[8,128]{1,0:T(8,128)S(1)}, u32[]{:S(2)}, u32[]{:S(2)}) %collective-permute-start.4) | collective-permute-done | bytes 4128 | tf_op jit(solution)/shard_map/ppermute | solution.py:401
  45.3 0.7 collective-permute-start.19
  46.0 0.0 collective-permute-done.12
  46.0 0.7 collective-permute-start.7
  46.6 0.0 collective-permute-done.16
  46.7 0.7 collective-permute-start.11
  47.3 0.0 collective-permute-done.8
  47.4 0.7 collective-permute-start.15
  48.0 0.0 collective-permute-done.15
  48.0 0.0 copy-start.15
  48.1 12.9 %collective-permute-start.5 = (f32[96,384]{1,0:T(8,128)S(1)}, f32[96,384]{1,0:T(8,128)S(1)}, u32[]{:S(2)}, u32[]{:S(2)}) collective-permute-start(f32[96,384]{1,0:T(8,128)S(1)} %get-tuple-element.123), channel_id=1, source_target_pairs={{0,4},{1,5},{2,6},{3,7},{4,0},{5,1},{6,2},{7,3},{8,12},{9,13},{10,... | collective-permute-start | bytes 442376 | tf_op jit(solution)/shard_map/ppermute | solution.py:394
  60.9 0.0 collective-permute-done.7
  60.9 0.6 copy-done.12
  61.5 0.2 collective-permute-start.9
  61.7 0.0 collective-permute-done.11
  61.7 0.7 collective-permute-start.10
  62.4 0.0 collective-permute-done.19
  62.4 0.6 copy-done.11
  63.0 0.7 collective-permute-start.14
  63.7 0.0 collective-permute-done.6
  63.7 0.7 collective-permute-start.18
  64.4 0.0 collective-permute-done.10
  64.4 11.4 %collective-permute-start.20 = (f32[184,384]{1,0:T(8,128)S(1)}, f32[184,384]{1,0:T(8,128)S(1)}, u32[]{:S(2)}, u32[]{:S(2)}) collective-permute-start(f32[184,384]{1,0:T(8,128)S(1)} %get-tuple-element.138), channel_id=1, source_target_pairs={{0,1},{1,0},{2,3},{3,2},{4,5},{5,4},{6,7},{7,6},{8,9},{9,8},{10,11... | collective-permute-start | bytes 847880 | tf_op jit(solution)/shard_map/ppermute | solution.py:394
  75.8 0.0 collective-permute-done.14
  75.8 0.0 collective-permute-start.21
  75.9 0.0 collective-permute-done.18
  75.9 0.0 copy-start.10
  75.9 0.6 copy-done.9
  76.5 3.5 %collective-permute-start.22 = (f32[184,384]{1,0:T(8,128)S(1)}, f32[184,384]{1,0:T(8,128)}, u32[]{:S(2)}, u32[]{:S(2)}) collective-permute-start(f32[184,384]{1,0:T(8,128)S(1)} %get-tuple-element.140), channel_id=1, source_target_pairs={{0,3},{1,2},{2,1},{3,0},{4,7},{5,6},{6,5},{7,4},{8,11},{9,10},{10,... | collective-permute-start | bytes 847880 | tf_op jit(solution)/shard_map/ppermute | solution.py:394
  80.0 0.0 collective-permute-done.5
  80.0 0.1 collective-permute-start.13
  80.1 0.0 collective-permute-done.9
  80.1 4.7 %collective-permute-start.17 = (f32[96,384]{1,0:T(8,128)S(1)}, f32[96,384]{1,0:T(8,128)}, u32[]{:S(2)}, u32[]{:S(2)}) collective-permute-start(f32[96,384]{1,0:T(8,128)S(1)} %get-tuple-element.135), channel_id=1, source_target_pairs={{0,7},{1,4},{2,5},{3,6},{4,3},{5,0},{6,1},{7,2},{8,15},{9,12},{10,... | collective-permute-start | bytes 442376 | tf_op jit(solution)/shard_map/ppermute | solution.py:394
  84.8 0.5 fusion.6
  86.6 0.6 slice_reduce_fusion
  87.2 0.0 copy-done.17
  87.9 2.9 %collective-permute-done.13 = f32[96,384]{1,0:T(8,128)} collective-permute-done((f32[96,384]{1,0:T(8,128)S(1)}, f32[96,384]{1,0:T(8,128)}, u32[]{:S(2)}, u32[]{:S(2)}) %collective-permute-start.13) | collective-permute-done | bytes 147488 | tf_op jit(solution)/shard_map/ppermute | solution.py:394
  90.8 0.5 collective-permute-done.17
  91.3 0.0 collective-permute-done.20
  91.3 0.0 collective-permute-done.21
  91.3 0.6 collective-permute-done.22
  92.0 6.2 %conditional.1 = ((f32[2,128,1024]{2,1,0:T(8,128)}, f32[2,128,1024]{2,1,0:T(8,128)}, f32[2,128,1024]{2,1,0:T(8,128)})) conditional(s32[]{:T(128)} %bitcast.16, (f32[8,128]{1,0:T(8,128)S(1)}, s32[2,128]{1,0:T(2,128)S(1)}, s32[2,128]{1,0:T(2,128)S(1)}, f32[96,384]{1,0:T(8,128)}, f32[56,384]{1,0:T(8,128)}, /*index=5*/f32[40,384]{1,0:T(8,128)}, ...), branch_computations={%region_0.0_spmd, %region_1.0_spmd} | conditional | flops 5100273664 | bytes 53839908 | solution.py:425
  92.0 6.2 %branch_0_fun.1 = (f32[2,128,1024]{2,1,0:T(8,128)}, f32[2,128,1024]{2,1,0:T(8,128)}, f32[2,128,1024]{2,1,0:T(8,128)}) custom-call(f32[8,128]{1,0:T(8,128)S(1)} %get-tuple-element.54.totals_ref, s32[2,128]{1,0:T(2,128)S(1)} %get-tuple-element.55.top_ref, s32[2,128]{1,0:T(2,128)S(1)} %get-tuple-element.56.bottom_ref, f32[96,384]{1,0:T(8,128)} %get-tuple-element.57.refs_0_, ...), custom_call_target="tpu_custom_call" | custom-call | flops 805306368 | bytes 6291456 | tf_op jit(solution)/shard_map/cond/branch_0_fun/pallas_call | solution.py:290
  (30 shorter events, 0.1 us)
Async XLA Ops:
  0.6 5.9 %copy-start.2 = (bf16[8,512,256]{2,1,0:T(8,128)(2,1)S(1)}, bf16[8,512,256]{2,1,0:T(8,128)(2,1)}, u32[]{:S(2)}) copy-start(bf16[8,512,256]{2,1,0:T(8,128)(2,1)} %constant.14.table_ref) | copy-start | bytes 6291460
  0.6 5.9 %copy-start.4 = (s32[2,128]{1,0:T(2,128)S(1)}, s32[2,128]{1,0:T(2,128)}, u32[]{:S(2)}) copy-start(s32[2,128]{1,0:T(2,128)} %bottom_ref.8) | copy-start | bytes 3076
  0.7 5.9 %copy-start.3 = (s32[2,128]{1,0:T(2,128)S(1)}, s32[2,128]{1,0:T(2,128)}, u32[]{:S(2)}) copy-start(s32[2,128]{1,0:T(2,128)} %top_ref.8) | copy-start | bytes 3076
  0.7 5.9 %copy-start = (bf16[2,4,128,2048]{3,2,1,0:T(8,128)(2,1)S(1)}, bf16[2,4,128,2048]{3,2,1,0:T(8,128)(2,1)}, u32[]{:S(2)}) copy-start(bf16[2,4,128,2048]{3,2,1,0:T(8,128)(2,1)} %x_ref.8) | copy-start | bytes 12582916
  5.9 41.5 %collective-permute-start.8 = (f32[32,384]{1,0:T(8,128)S(1)}, f32[32,384]{1,0:T(8,128)S(1)}, u32[]{:S(2)}, u32[]{:S(2)}) collective-permute-start(f32[32,384]{1,0:T(8,128)S(1)} %get-tuple-element.126), channel_id=1, source_target_pairs={{7,3},{15,11},{23,19},{31,27}} | collective-permute-start | bytes 147464 | tf_op jit(solution)/shard_map/ppermute | solution.py:394
  8.8 37.1 %collective-permute-start.12 = (f32[24,384]{1,0:T(8,128)S(1)}, f32[24,384]{1,0:T(8,128)S(1)}, u32[]{:S(2)}, u32[]{:S(2)}) collective-permute-start(f32[24,384]{1,0:T(8,128)S(1)} %get-tuple-element.130), channel_id=1, source_target_pairs={{6,3},{14,11},{22,19},{30,27}} | collective-permute-start | bytes 110600 | tf_op jit(solution)/shard_map/ppermute | solution.py:394
  14.5 32.1 %collective-permute-start.16 = (f32[24,384]{1,0:T(8,128)S(1)}, f32[24,384]{1,0:T(8,128)S(1)}, u32[]{:S(2)}, u32[]{:S(2)}) collective-permute-start(f32[24,384]{1,0:T(8,128)S(1)} %get-tuple-element.134), channel_id=1, source_target_pairs={{5,3},{13,11},{21,19},{29,27}} | collective-permute-start | bytes 110600 | tf_op jit(solution)/shard_map/ppermute | solution.py:394
  24.9 1.3 %collective-permute-start = (f32[8,128]{1,0:T(8,128)S(1)}, f32[8,128]{1,0:T(8,128)S(1)}, u32[]{:S(2)}, u32[]{:S(2)}) collective-permute-start(f32[8,128]{1,0:T(8,128)S(1)} %get-tuple-element.122), channel_id=1, source_target_pairs={{0,8},{8,0},{16,24},{24,16},{1,9},{9,1},{17,25},{25,17},{2,10},{10... | collective-permute-start | bytes 12296 | tf_op jit(solution)/shard_map/ppermute | solution.py:401
  26.3 4.4 %collective-permute-start.1 = (f32[8,128]{1,0:T(8,128)S(1)}, f32[8,128]{1,0:T(8,128)S(1)}, u32[]{:S(2)}, u32[]{:S(2)}) collective-permute-start(f32[8,128]{1,0:T(8,128)S(1)} %add.15), channel_id=1, source_target_pairs={{0,16},{8,24},{16,0},{24,8},{1,17},{9,25},{17,1},{25,9},{2,18},{10... | collective-permute-start | bytes 12296 | tf_op jit(solution)/shard_map/ppermute | solution.py:401
  30.7 3.6 %collective-permute-start.2 = (f32[8,128]{1,0:T(8,128)S(1)}, f32[8,128]{1,0:T(8,128)S(1)}, u32[]{:S(2)}, u32[]{:S(2)}) collective-permute-start(f32[8,128]{1,0:T(8,128)S(1)} %add.16), channel_id=1, source_target_pairs={{0,1},{1,0},{2,3},{3,2},{4,5},{5,4},{6,7},{7,6},{8,9},{9,8},{10,11... | collective-permute-start | bytes 12296 | tf_op jit(solution)/shard_map/ppermute | solution.py:401
  32.7 31.0 %collective-permute-start.6 = (f32[56,384]{1,0:T(8,128)S(1)}, f32[56,384]{1,0:T(8,128)S(1)}, u32[]{:S(2)}, u32[]{:S(2)}) collective-permute-start(f32[56,384]{1,0:T(8,128)S(1)} %get-tuple-element.124), channel_id=1, source_target_pairs={{5,1},{6,2},{7,3},{13,9},{14,10},{15,11},{21,17},{22,18},{23,19},{... | collective-permute-start | bytes 258056 | tf_op jit(solution)/shard_map/ppermute | solution.py:394
  34.3 5.0 %collective-permute-start.3 = (f32[8,128]{1,0:T(8,128)S(1)}, f32[8,128]{1,0:T(8,128)S(1)}, u32[]{:S(2)}, u32[]{:S(2)}) collective-permute-start(f32[8,128]{1,0:T(8,128)S(1)} %add.17), channel_id=1, source_target_pairs={{0,2},{1,3},{2,0},{3,1},{4,6},{5,7},{6,4},{7,5},{8,10},{9,11},{10,... | collective-permute-start | bytes 12296 | tf_op jit(solution)/shard_map/ppermute | solution.py:401
  39.3 6.0 %collective-permute-start.4 = (f32[8,128]{1,0:T(8,128)S(1)}, f32[8,128]{1,0:T(8,128)S(1)}, u32[]{:S(2)}, u32[]{:S(2)}) collective-permute-start(f32[8,128]{1,0:T(8,128)S(1)} %add.18), channel_id=1, source_target_pairs={{0,4},{1,5},{2,6},{3,7},{4,0},{5,1},{6,2},{7,3},{8,12},{9,13},{10,... | collective-permute-start | bytes 12296 | tf_op jit(solution)/shard_map/ppermute | solution.py:401
  45.3 17.1 %collective-permute-start.19 = (f32[48,384]{1,0:T(8,128)S(1)}, f32[48,384]{1,0:T(8,128)S(1)}, u32[]{:S(2)}, u32[]{:S(2)}) collective-permute-start(f32[48,384]{1,0:T(8,128)S(1)} %get-tuple-element.137), channel_id=1, source_target_pairs={{4,3},{7,2},{12,11},{15,10},{20,19},{23,18},{28,27},{31,26}} | collective-permute-start | bytes 221192 | tf_op jit(solution)/shard_map/ppermute | solution.py:394
  46.0 40.7 %copy-start.16 = (f32[24,384]{1,0:T(8,128)}, f32[24,384]{1,0:T(8,128)S(1)}, u32[]{:S(2)}) copy-start(f32[24,384]{1,0:T(8,128)S(1)} %collective-permute-done.12) | copy-start | bytes 110596
  46.0 14.9 %collective-permute-start.7 = (f32[40,384]{1,0:T(8,128)S(1)}, f32[40,384]{1,0:T(8,128)S(1)}, u32[]{:S(2)}, u32[]{:S(2)}) collective-permute-start(f32[40,384]{1,0:T(8,128)S(1)} %get-tuple-element.125), channel_id=1, source_target_pairs={{6,2},{7,3},{14,10},{15,11},{22,18},{23,19},{30,26},{31,27}} | collective-permute-start | bytes 184328 | tf_op jit(solution)/shard_map/ppermute | solution.py:394
  46.7 40.6 %copy-start.17 = (f32[24,384]{1,0:T(8,128)}, f32[24,384]{1,0:T(8,128)S(1)}, u32[]{:S(2)}) copy-start(f32[24,384]{1,0:T(8,128)S(1)} %collective-permute-done.16) | copy-start | bytes 110596
  46.7 15.0 %collective-permute-start.11 = (f32[40,384]{1,0:T(8,128)S(1)}, f32[40,384]{1,0:T(8,128)S(1)}, u32[]{:S(2)}, u32[]{:S(2)}) collective-permute-start(f32[40,384]{1,0:T(8,128)S(1)} %get-tuple-element.129), channel_id=1, source_target_pairs={{5,2},{6,3},{13,10},{14,11},{21,18},{22,19},{29,26},{30,27}} | collective-permute-start | bytes 184328 | tf_op jit(solution)/shard_map/ppermute | solution.py:394
  47.4 38.6 %copy-start.14 = (f32[32,384]{1,0:T(8,128)}, f32[32,384]{1,0:T(8,128)S(1)}, u32[]{:S(2)}) copy-start(f32[32,384]{1,0:T(8,128)S(1)} %collective-permute-done.8) | copy-start | bytes 147460
  47.4 0.7 collective-permute-start.15
  48.0 37.9 %copy-start.15 = (f32[32,384]{1,0:T(8,128)}, f32[32,384]{1,0:T(8,128)S(1)}, u32[]{:S(2)}) copy-start(f32[32,384]{1,0:T(8,128)S(1)} %collective-permute-done.15) | copy-start | bytes 147460
  48.1 31.9 %collective-permute-start.5 = (f32[96,384]{1,0:T(8,128)S(1)}, f32[96,384]{1,0:T(8,128)S(1)}, u32[]{:S(2)}, u32[]{:S(2)}) collective-permute-start(f32[96,384]{1,0:T(8,128)S(1)} %get-tuple-element.123), channel_id=1, source_target_pairs={{0,4},{1,5},{2,6},{3,7},{4,0},{5,1},{6,2},{7,3},{8,12},{9,13},{10,... | collective-permute-start | bytes 442376 | tf_op jit(solution)/shard_map/ppermute | solution.py:394
  60.9 0.6 copy-start.12
  61.5 18.6 %collective-permute-start.9 = (f32[96,384]{1,0:T(8,128)S(1)}, f32[96,384]{1,0:T(8,128)S(1)}, u32[]{:S(2)}, u32[]{:S(2)}) collective-permute-start(f32[96,384]{1,0:T(8,128)S(1)} %get-tuple-element.127), channel_id=1, source_target_pairs={{0,5},{1,6},{2,7},{3,4},{4,1},{5,2},{6,3},{7,0},{8,13},{9,14},{10,... | collective-permute-start | bytes 442376 | tf_op jit(solution)/shard_map/ppermute | solution.py:394
  61.7 0.7 copy-start.13
  61.7 2.7 %collective-permute-start.10 = (f32[56,384]{1,0:T(8,128)S(1)}, f32[56,384]{1,0:T(8,128)S(1)}, u32[]{:S(2)}, u32[]{:S(2)}) collective-permute-start(f32[56,384]{1,0:T(8,128)S(1)} %get-tuple-element.128), channel_id=1, source_target_pairs={{4,1},{5,2},{6,3},{12,9},{13,10},{14,11},{20,17},{21,18},{22,19},{... | collective-permute-start | bytes 258056 | tf_op jit(solution)/shard_map/ppermute | solution.py:394
  62.4 0.6 copy-start.11
  63.0 12.8 %collective-permute-start.14 = (f32[56,384]{1,0:T(8,128)S(1)}, f32[56,384]{1,0:T(8,128)S(1)}, u32[]{:S(2)}, u32[]{:S(2)}) collective-permute-start(f32[56,384]{1,0:T(8,128)S(1)} %get-tuple-element.132), channel_id=1, source_target_pairs={{4,2},{5,3},{7,1},{12,10},{13,11},{15,9},{20,18},{21,19},{23,17},{... | collective-permute-start | bytes 258056 | tf_op jit(solution)/shard_map/ppermute | solution.py:394
  63.7 21.6 %copy-start.7 = (f32[56,384]{1,0:T(8,128)}, f32[56,384]{1,0:T(8,128)S(1)}, u32[]{:S(2)}) copy-start(f32[56,384]{1,0:T(8,128)S(1)} %collective-permute-done.6) | copy-start | bytes 258052
  63.7 12.2 %collective-permute-start.18 = (f32[56,384]{1,0:T(8,128)S(1)}, f32[56,384]{1,0:T(8,128)S(1)}, u32[]{:S(2)}, u32[]{:S(2)}) collective-permute-start(f32[56,384]{1,0:T(8,128)S(1)} %get-tuple-element.136), channel_id=1, source_target_pairs={{4,3},{6,1},{7,2},{12,11},{14,9},{15,10},{20,19},{22,17},{23,18},{... | collective-permute-start | bytes 258056 | tf_op jit(solution)/shard_map/ppermute | solution.py:394
  64.4 20.9 %copy-start.8 = (f32[56,384]{1,0:T(8,128)}, f32[56,384]{1,0:T(8,128)S(1)}, u32[]{:S(2)}) copy-start(f32[56,384]{1,0:T(8,128)S(1)} %collective-permute-done.10) | copy-start | bytes 258052
  64.4 26.9 %collective-permute-start.20 = (f32[184,384]{1,0:T(8,128)S(1)}, f32[184,384]{1,0:T(8,128)S(1)}, u32[]{:S(2)}, u32[]{:S(2)}) collective-permute-start(f32[184,384]{1,0:T(8,128)S(1)} %get-tuple-element.138), channel_id=1, source_target_pairs={{0,1},{1,0},{2,3},{3,2},{4,5},{5,4},{6,7},{7,6},{8,9},{9,8},{10,11... | collective-permute-start | bytes 847880 | tf_op jit(solution)/shard_map/ppermute | solution.py:394
  75.8 0.6 copy-start.9
  75.8 15.5 %collective-permute-start.21 = (f32[184,384]{1,0:T(8,128)S(1)}, f32[184,384]{1,0:T(8,128)}, u32[]{:S(2)}, u32[]{:S(2)}) collective-permute-start(f32[184,384]{1,0:T(8,128)S(1)} %get-tuple-element.139), channel_id=1, source_target_pairs={{0,2},{1,3},{2,0},{3,1},{4,6},{5,7},{6,4},{7,5},{8,10},{9,11},{10,... | collective-permute-start | bytes 847880 | tf_op jit(solution)/shard_map/ppermute | solution.py:394
  75.9 10.1 %copy-start.10 = (f32[56,384]{1,0:T(8,128)}, f32[56,384]{1,0:T(8,128)S(1)}, u32[]{:S(2)}) copy-start(f32[56,384]{1,0:T(8,128)S(1)} %collective-permute-done.18) | copy-start | bytes 258052
  76.5 15.5 %collective-permute-start.22 = (f32[184,384]{1,0:T(8,128)S(1)}, f32[184,384]{1,0:T(8,128)}, u32[]{:S(2)}, u32[]{:S(2)}) collective-permute-start(f32[184,384]{1,0:T(8,128)S(1)} %get-tuple-element.140), channel_id=1, source_target_pairs={{0,3},{1,2},{2,1},{3,0},{4,7},{5,6},{6,5},{7,4},{8,11},{9,10},{10,... | collective-permute-start | bytes 847880 | tf_op jit(solution)/shard_map/ppermute | solution.py:394
  80.0 4.8 %copy-start.5 = (f32[96,384]{1,0:T(8,128)}, f32[96,384]{1,0:T(8,128)S(1)}, u32[]{:S(2)}) copy-start(f32[96,384]{1,0:T(8,128)S(1)} %collective-permute-done.5) | copy-start | bytes 442372
  80.0 10.8 %collective-permute-start.13 = (f32[96,384]{1,0:T(8,128)S(1)}, f32[96,384]{1,0:T(8,128)}, u32[]{:S(2)}, u32[]{:S(2)}) collective-permute-start(f32[96,384]{1,0:T(8,128)S(1)} %get-tuple-element.131), channel_id=1, source_target_pairs={{0,6},{1,7},{2,4},{3,5},{4,2},{5,3},{6,0},{7,1},{8,14},{9,15},{10,... | collective-permute-start | bytes 442376 | tf_op jit(solution)/shard_map/ppermute | solution.py:394
  80.1 5.2 %copy-start.6 = (f32[96,384]{1,0:T(8,128)}, f32[96,384]{1,0:T(8,128)S(1)}, u32[]{:S(2)}) copy-start(f32[96,384]{1,0:T(8,128)S(1)} %collective-permute-done.9) | copy-start | bytes 442372
  80.1 11.2 %collective-permute-start.17 = (f32[96,384]{1,0:T(8,128)S(1)}, f32[96,384]{1,0:T(8,128)}, u32[]{:S(2)}, u32[]{:S(2)}) collective-permute-start(f32[96,384]{1,0:T(8,128)S(1)} %get-tuple-element.135), channel_id=1, source_target_pairs={{0,7},{1,4},{2,5},{3,6},{4,3},{5,0},{6,1},{7,2},{8,15},{9,12},{10,... | collective-permute-start | bytes 442376 | tf_op jit(solution)/shard_map/ppermute | solution.py:394
where the time goes:
time: 99.8 us; the launch traced here: 99.3 us
  starting transfers between devices  53.2 us (53%)
  Pallas kernels  28.4 us (28%)
  waiting for transfers between devices  10.6 us (11%)
  between operations  4.11 us (4%)
  local copies, waits for them, and re-layouts  2.42 us (2%)
    ppermute x18, starting transfers between devices, sparse_body(): message = lax.ppermute(message, 'ascan', pairs)  40 us
    pallas_call x4, Pallas kernels, send(): pl.pallas_call(functools.partial(send_kernel, peers, messages, rooms), ou...  22.2 us
    ppermute x5, starting transfers between devices, sparse_body(): lax.ppermute(totals, axis, [(s, s ^ stride) for s in range(length)])  13.2 us
    ppermute x5, waiting for transfers between devices, sparse_body(): lax.ppermute(totals, axis, [(s, s ^ stride) for s in range(length)])  6.53 us
    pallas_call x1, Pallas kernels, receive(): pl.pallas_call(functools.partial(receive_kernel, peers, messages), out_sh...  6.19 us
    ppermute x18, waiting for transfers between devices, sparse_body(): message = lax.ppermute(message, 'ascan', pairs)  4.09 us
  transfers between devices with their start and end apart: 23, of which 8 were waited for; matrix products, arithmetic and copies ran while one was open for 1% of the time, Pallas kernels for 17%

commit v1 on v0

--- a/solution.py
+++ b/solution.py
@@ -20,7 +20,12 @@
 FLOOR = 0.05 * BAND_BINS
 VARIANCE_SCALE = 0.1
 HEAD = 2
+MERGE = 44
+UNROLL = 4
 MAPS = 3
+
+
+VMEM = pl.BlockSpec(memory_space=pltpu.VMEM)
 
 
 def table_values():
@@ -44,14 +49,14 @@
 def moments_rows(profile_ref, buf, out_ref, slot, scan, ascans, begin, end):
     tiny = jnp.float32(np.finfo(np.float32).tiny)
     step = 8
-    for start in range(begin, end, step):
+    for start in range(begin, end, step) if isinstance(begin, int) else [pl.multiple_of(begin, step)]:
         sim = amp = var1 = var2 = None
         for band in range(BANDS):
             power, amplitude = [], []
             for repeat in range(REPEATS):
                 base = repeat * ascans + start
-                re = profile_ref[buf, band, base : base + step, :TILE]
-                im = profile_ref[buf, band, base : base + step, TILE:]
+                re = profile_ref[buf, band, pl.ds(base, step), :TILE]
+                im = profile_ref[buf, band, pl.ds(base, step), TILE:]
                 p = re * re + im * im
                 power.append(p)
                 amplitude.append(p * lax.rsqrt(jnp.maximum(p, tiny)))
@@ -121,44 +126,75 @@
     return me ^ index if kind == "near" else index
 
 
-def send_kernel(peers, messages, rooms, x_ref, table_ref, top_ref, bottom_ref, stats_in, *refs):
-    outs = refs[: sum(len(m) for m in messages)]
-    stats_ref, profile_ref, maps_ref = refs[len(outs) :]
+def send_kernel(peers, messages, rooms, staged, x_ref, table_ref, top_ref, bottom_ref, stats_in, *refs):
+    count = sum(len(m) for m in messages)
+    outs = refs[:count]
+    stats_ref, *rest = refs[count:]
+    if staged:
+        x_vmem, table_vmem, *rest = rest
+    profile_ref, maps_ref, *rest = rest
     slots = len(peers)
     scans, _, ascans, _ = x_ref.shape
     me = lax.axis_index("ascan")
     half = lax.axis_size("ascan") // 2
     tiles = [jnp.asarray(peer_target(p, me, half), jnp.int32) for p in peers]
 
-    def pick(slot):
-        if isinstance(slot, int):
-            return tiles[slot]
+    def lanes_of(band):
+        return slice(band * BAND_BINS, (band + 1) * BAND_BINS)
+
+    if staged:
+        x_sem, table_sem = rest
+
+        def x_copy(scan):
+            return pltpu.make_async_copy(x_ref.at[scan], x_vmem.at[scan], x_sem.at[scan])
+
+        first = tiles[0]
+
+        def table_copy(index):
+            tile = (first + index) & (TILES - 1)
+            return pltpu.make_async_copy(
+                table_ref.at[tile], table_vmem.at[tile], table_sem.at[index]
+            )
+
+        table_copy(0).start()
+        for scan in range(scans):
+            x_copy(scan).start()
+        for index in range(1, TILES):
+            table_copy(index).start()
+        x_used, table_used = x_vmem, table_vmem
+    else:
+        x_used, table_used = x_ref, table_ref
+
+    def product(weights, slot, scan, buf, band):
+        if staged and slot == 0 and band == 0:
+            x_copy(scan).wait()
+        x = x_used[scan, :, :, lanes_of(band)].reshape(REPEATS * ascans, BAND_BINS)
+        profile_ref[buf, band] = jnp.dot(x, weights, preferred_element_type=jnp.float32)
+
+    def weights_of(slot):
         chosen = tiles[0]
         for i in range(1, slots):
             chosen = jnp.where(slot == i, tiles[i], chosen)
-        return chosen
-
-    def product(weights, scan, buf, band):
-        lanes = slice(band * BAND_BINS, (band + 1) * BAND_BINS)
-        x = x_ref[scan, :, :, lanes].reshape(REPEATS * ascans, BAND_BINS)
-        profile_ref[buf, band] = jnp.dot(x, weights, preferred_element_type=jnp.float32)
+        return table_used[chosen]
 
     def both(following, current):
-        weights = table_ref[pick(following[0])] if following else None
+        if following:
+            if staged and following == (0, 0):
+                table_copy(0).wait()
+            weights = weights_of(following[0])
         share = ascans // BANDS
         for band in range(BANDS):
             if following:
-                product(weights, following[1], following[1] % 2, band)
+                product(weights, following[0], following[1], following[1] % 2, band)
             if current:
                 moments_rows(
                     profile_ref, current[1] % 2, maps_ref, *current, ascans, band * share, (band + 1) * share
                 )
 
-    if slots == 1:
-        both((0, 0), None)
-        for scan in range(scans - 1):
-            both((0, scan + 1), (0, scan))
-        both(None, (0, scans - 1))
+    if slots <= UNROLL:
+        order = [(slot, scan) for slot in range(slots) for scan in range(scans)]
+        for following, current in zip(order + [None], [None] + order):
+            both(following, current)
     else:
         both((0, 0), None)
 
@@ -170,6 +206,9 @@
 
         lax.fori_loop(0, slots, step, 0)
 
+    if staged:
+        for index in range(1, TILES):
+            table_copy(index).wait()
     top = flat_rows(top_ref[...])
     bottom = flat_rows(bottom_ref[...])
     rows = top.shape[1]
@@ -204,10 +243,61 @@
     )
 
 
-VMEM = pl.BlockSpec(memory_space=pltpu.VMEM)
-
-
-def send(peers, spectra, tables, top, bottom, stats, messages, rooms):
+def dense_send_kernel(x_ref, table_ref, top_ref, bottom_ref, out_ref, profile_ref, maps_ref):
+    scans, _, ascans, _ = x_ref.shape
+    top = flat_rows(top_ref[...])
+    bottom = flat_rows(bottom_ref[...])
+    rows = top.shape[1]
+
+    def step(tile, carry):
+        weights = table_ref[tile]
+
+        def scan_step(scan, inner):
+            for band in range(BANDS):
+                x = x_ref[scan, :, :, band * BAND_BINS : (band + 1) * BAND_BINS]
+                profile_ref[0, band] = jnp.dot(
+                    x.reshape(REPEATS * ascans, BAND_BINS), weights, preferred_element_type=jnp.float32
+                )
+
+            def rows_step(chunk, last):
+                moments_rows(profile_ref, 0, maps_ref, 0, scan, ascans, chunk * 8, chunk * 8 + 8)
+                return last
+
+            return lax.fori_loop(0, ascans // 8, rows_step, inner)
+
+        lax.fori_loop(0, scans, scan_step, 0)
+        high, low = split(maps_ref[0])
+        mask = (top <= tile) & (tile < bottom)
+        same = lax.broadcasted_iota(jnp.int32, (rows, rows), 0) == lax.broadcasted_iota(
+            jnp.int32, (rows, rows), 1
+        )
+        choice = jnp.where(same & mask, 1.0, 0.0).astype(jnp.bfloat16)
+        out_ref[tile] = jnp.dot(choice, high, preferred_element_type=jnp.float32) + jnp.dot(
+            choice, low, preferred_element_type=jnp.float32
+        )
+        return carry
+
+    lax.fori_loop(0, TILES, step, 0)
+
+
+def dense_send(spectra, tables, top, bottom):
+    scans, repeats, ascans, _ = spectra.shape
+    rows = scans * ascans
+    return pl.pallas_call(
+        dense_send_kernel,
+        out_shape=jax.ShapeDtypeStruct((TILES, rows, MAPS * TILE), jnp.float32),
+        in_specs=[VMEM] * 4,
+        out_specs=VMEM,
+        scratch_shapes=[
+            pltpu.VMEM((1, BANDS, repeats * ascans, 2 * TILE), jnp.float32),
+            pltpu.VMEM((1, rows, MAPS * TILE), jnp.float32),
+        ],
+        compiler_params=pltpu.CompilerParams(vmem_limit_bytes=32 * 1024 * 1024),
+        name="dense_send",
+    )(spectra, tables, top, bottom)
+
+
+def send(peers, spectra, tables, top, bottom, stats, messages, rooms, staged=False):
     scans, repeats, ascans, bins = spectra.shape
     assert scans % 2 == 0
     rows = scans * ascans
@@ -217,22 +307,61 @@
         for _, size, _, _ in parts
     ]
     shapes.append(jax.ShapeDtypeStruct((8, TILE), jnp.float32))
+    if staged:
+        assert len(peers) == 1
+        shapes.append(jax.ShapeDtypeStruct(spectra.shape, spectra.dtype))
+        shapes.append(jax.ShapeDtypeStruct(tables.shape, tables.dtype))
+    scratch = [
+        pltpu.VMEM((2, BANDS, repeats * ascans, 2 * TILE), jnp.float32),
+        pltpu.VMEM((len(peers), rows, MAPS * TILE), jnp.float32),
+    ]
+    specs = [VMEM] * 5
+    if staged:
+        scratch += [
+            pltpu.SemaphoreType.DMA((scans,)),
+            pltpu.SemaphoreType.DMA((TILES,)),
+        ]
+        specs[:2] = [pl.BlockSpec(memory_space=pltpu.HBM)] * 2
     return pl.pallas_call(
-        functools.partial(send_kernel, peers, messages, rooms),
+        functools.partial(send_kernel, peers, messages, rooms, staged),
         out_shape=shapes,
-        in_specs=[VMEM] * 5,
+        in_specs=specs,
         out_specs=[VMEM] * len(shapes),
-        scratch_shapes=[
-            pltpu.VMEM((2, BANDS, repeats * ascans, 2 * TILE), jnp.float32),
-            pltpu.VMEM((len(peers), rows, MAPS * TILE), jnp.float32),
-        ],
+        scratch_shapes=scratch,
         cost_estimate=pl.CostEstimate(
             flops=2 * rows * repeats * bins * 2 * TILE * len(peers),
             bytes_accessed=2 * spectra.size,
             transcendentals=0,
         ),
-        compiler_params=pltpu.CompilerParams(vmem_limit_bytes=32 * 1024 * 1024),
+        compiler_params=pltpu.CompilerParams(vmem_limit_bytes=18 * 1024 * 1024),
     )(spectra, tables, top, bottom, stats)
+
+
+def mean_scale(totals):
+    flow = jnp.sum(totals[0:1, :], axis=1, keepdims=True)
+    return (totals[1:2, 0:1] * TILE) / (3.0 * flow)
+
+
+def smooth(decorrelation_ref, angiogram_ref, scale):
+    scans, _, total = angiogram_ref.shape
+    step = 8
+    for scan in range(scans):
+        for start in range(0, TILE, step):
+            d = decorrelation_ref[scan, start : start + step, :]
+            lane = lax.broadcasted_iota(jnp.int32, d.shape, 1)
+            left = jnp.where(lane == 0, 0.0, pltpu.roll(d, 1, 1))
+            right = jnp.where(lane == total - 1, 0.0, pltpu.roll(d, total - 1, 1))
+            angiogram_ref[scan, start : start + step, :] = ((left + d) + right) * scale
+
+
+def place(piece, choice):
+    result = None
+    for part in split(piece):
+        term = lax.dot_general(
+            part, choice, (((0,), (0,)), ((), ())), preferred_element_type=jnp.float32
+        )
+        result = term if result is None else result + term
+    return result
 
 
 def receive_kernel(peers, messages, totals_ref, top_ref, bottom_ref, *refs):
@@ -240,7 +369,6 @@
     ins = refs[:count]
     angiogram_ref, structure_ref, speckle_ref, decorrelation_ref = refs[count:]
     scans = angiogram_ref.shape[0]
-    total = angiogram_ref.shape[2]
     own_top = flat_rows(top_ref[...])
     own_bottom = flat_rows(bottom_ref[...])
     rows = own_top.shape[1]
@@ -260,11 +388,8 @@
         result = None
         for piece, (first, size, carried, header) in zip(pieces, parts):
             choice = chooser(jnp.where(rank < first + carried, rank, -1), first, size)
-            for part in split(piece[...]):
-                term = lax.dot_general(
-                    part, choice, (((0,), (0,)), ((), ())), preferred_element_type=jnp.float32
-                )
-                result = term if result is None else result + term
+            term = place(piece[...], choice)
+            result = term if result is None else result + term
         origin = jnp.asarray(peer_origin(peer, me, half), jnp.int32)
         lanes = pl.ds(pl.multiple_of(origin * ascans, ascans), ascans)
         for scan in range(scans):
@@ -272,34 +397,49 @@
             decorrelation_ref[scan, :, lanes] = result[0:TILE, columns]
             structure_ref[scan, :, lanes] = result[TILE : 2 * TILE, columns]
             speckle_ref[scan, :, lanes] = result[2 * TILE :, columns]
-    flow = jnp.sum(totals_ref[0:1, :], axis=1, keepdims=True)
-    scale = (totals_ref[1:2, 0:1] * TILE) / (3.0 * flow)
-    step = 8
-    for scan in range(scans):
-        for start in range(0, TILE, step):
-            d = decorrelation_ref[scan, start : start + step, :]
-            lane = lax.broadcasted_iota(jnp.int32, d.shape, 1)
-            left = jnp.where(lane == 0, 0.0, pltpu.roll(d, 1, 1))
-            right = jnp.where(lane == total - 1, 0.0, pltpu.roll(d, total - 1, 1))
-            angiogram_ref[scan, start : start + step, :] = ((left + d) + right) * scale
-
-
-def receive(peers, totals, top, bottom, pieces, messages, members):
-    scans, ascans = top.shape
-    shape = jax.ShapeDtypeStruct((scans, TILE, members * ascans), jnp.float32)
-    return pl.pallas_call(
-        functools.partial(receive_kernel, peers, messages),
-        out_shape=[shape] * MAPS,
-        in_specs=[VMEM] * (3 + len(pieces)),
-        out_specs=[VMEM] * MAPS,
-        scratch_shapes=[pltpu.VMEM(shape.shape, jnp.float32)],
-        cost_estimate=pl.CostEstimate(
-            flops=2 * 2 * scans * ascans * 256 * MAPS * TILE * members,
-            bytes_accessed=8 * MAPS * scans * TILE * members * ascans,
-            transcendentals=0,
-        ),
-        compiler_params=pltpu.CompilerParams(vmem_limit_bytes=32 * 1024 * 1024),
-    )(totals, top, bottom, *pieces)
+    smooth(decorrelation_ref, angiogram_ref, mean_scale(totals_ref[...]))
+
+
+def dense_receive_kernel(totals_ref, pieces_ref, angiogram_ref, structure_ref, speckle_ref, decorrelation_ref):
+    members, rows, _ = pieces_ref.shape
+    scans = angiogram_ref.shape[0]
+    ascans = rows // scans
+    same = lax.broadcasted_iota(jnp.int32, (rows, rows), 0) == lax.broadcasted_iota(
+        jnp.int32, (rows, rows), 1
+    )
+    choice = jnp.where(same, 1.0, 0.0).astype(jnp.bfloat16)
+
+    def step(source, carry):
+        result = place(pieces_ref[source], choice)
+        lanes = pl.ds(pl.multiple_of(source * ascans, ascans), ascans)
+        for scan in range(scans):
+            columns = slice(scan * ascans, (scan + 1) * ascans)
+            decorrelation_ref[scan, :, lanes] = result[0:TILE, columns]
+            structure_ref[scan, :, lanes] = result[TILE : 2 * TILE, columns]
+            speckle_ref[scan, :, lanes] = result[2 * TILE :, columns]
+        return carry
+
+    lax.fori_loop(0, members, step, 0)
+    smooth(decorrelation_ref, angiogram_ref, mean_scale(totals_ref[...]))
+
+
+def result_call(kernel, operands, scans, total):
+    shape = jax.ShapeDtypeStruct((scans, TILE, total), jnp.float32)
+    return tuple(
+        pl.pallas_call(
+            kernel,
+            out_shape=[shape] * MAPS,
+            in_specs=[VMEM] * len(operands),
+            out_specs=[VMEM] * MAPS,
+            scratch_shapes=[pltpu.VMEM(shape.shape, jnp.float32)],
+            cost_estimate=pl.CostEstimate(
+                flops=1024 * scans * MAPS * TILE * total,
+                bytes_accessed=8 * MAPS * scans * TILE * total,
+                transcendentals=0,
+            ),
+            compiler_params=pltpu.CompilerParams(vmem_limit_bytes=24 * 1024 * 1024),
+        )(*operands)
+    )
 
 
 def capacities(members, scans, ascans):
@@ -319,14 +459,12 @@
 
 def plan_levels(caps, matching, merge):
     need = [int(caps[s, d]) + (HEAD if s != d else 0) for s, d in matching]
-    base = sorted(need)[len(need) // 2]
+    base = -(-sorted(need)[len(need) // 2] // 8) * 8
     need = [max(n, base) for n in need]
     marks = []
-    for value in sorted(set(-(-n // 8) * 8 for n in need)):
-        if len(marks) > 1 and value - marks[-1] < merge:
-            marks[-1] = value
-        else:
-            marks.append(value)
+    for value in sorted(set(-(-n // 8) * 8 for n in need), reverse=True):
+        if not marks or value == base or marks[0] - value >= merge:
+            marks.insert(0, value)
     messages, pair_lists, room, below = [], [], [0] * len(need), 0
     for mark in marks:
         pairs = [pair for pair, n in zip(matching, need) if n > below]
@@ -351,14 +489,15 @@
     def pairs_of(peer):
         return [(s, int(peer_target(peer, s, half))) for s in range(members)]
 
-    plans = {peer: plan_levels(caps, pairs_of(peer), 24) for peer in far}
+    plans = {peer: plan_levels(caps, pairs_of(peer), MERGE) for peer in far}
     widest = max(int(caps[s, d]) for peer in near for s, d in pairs_of(peer))
-    size = min(-(-(widest + HEAD) // 8) * 8, rows)
+    head = HEAD
+    size = -(-(widest + head) // 8) * 8
     for peer in near:
         plans[peer] = (
-            ((0, size, size - HEAD, True),),
+            ((0, size, size - head, True),),
             [pairs_of(peer)],
-            (size - HEAD,) * members,
+            (size - head,) * members,
         )
     plans[own] = (((0, rows, rows, False),), [None], (rows,) * members)
     return plans, far, near, own
@@ -366,64 +505,72 @@
 
 def sparse_body(members, spectra, top, bottom):
     scans, _, ascans, _ = spectra.shape
-    rows = scans * ascans
-    half = members // 2
     tables = tile_tables(TILE)
     plans, far, near, own = exchange_plans(members, scans, ascans)
     stats = jnp.zeros((8, TILE), jnp.float32)
     sent = {}
-    for number, group in enumerate((far[:1], far[1:2], far[2:], near + [own])):
-        *out, stats = send(
-            group,
-            spectra,
-            tables,
-            top,
-            bottom,
-            stats,
-            [plans[p][0] for p in group],
-            [plans[p][2] for p in group],
+    spectra_here, tables_here = spectra, tables
+    peers = far + near + [own]
+    for number, group in enumerate(tile_groups(far, near, own)):
+        out = list(
+            send(
+                group,
+                spectra_here,
+                tables_here,
+                top,
+                bottom,
+                stats,
+                [plans[p][0] for p in group],
+                [plans[p][2] for p in group],
+                staged=number == 0,
+            )
         )
         for peer in group:
             for level in range(len(plans[peer][0])):
                 sent[peer, level] = out.pop(0)
-    received = []
-    for peer in far + near + [own]:
+        stats = out.pop(0)
+        if number == 0:
+            spectra_here, tables_here = out
+    length = lax.axis_size("scan")
+    hops = [("ascan", flipped(members, 1))]
+    hops += [("scan", flipped(length, stride)) for stride in strides(length)]
+    for axis, pairs in hops:
+        stats = stats + lax.ppermute(stats, axis, pairs)
+    received, shares = [], [stats]
+    for peer in peers:
         for level, pairs in enumerate(plans[peer][1]):
             message = sent[peer, level]
             if pairs is not None:
                 message = lax.ppermute(message, "ascan", pairs)
             received.append(message)
-    number = 0
-    totals = stats
-    for axis, length in (("scan", lax.axis_size("scan")), ("ascan", members)):
-        stride = 1
-        while stride < length:
-            totals = totals + lax.ppermute(totals, axis, [(s, s ^ stride) for s in range(length)])
-            stride *= 2
-            number += 1
+    for bits in range(2, members, 2):
+        shares.append(lax.ppermute(stats, "ascan", flipped(members, bits)))
+    totals = functools.reduce(jnp.add, shares)
     mean_flow = jnp.sum(totals[0]) / (totals[1, 0] * TILE)
 
     def quick(received):
-        peers = far + near + [own]
-        messages = [plans[p][0] for p in peers]
-        return tuple(receive(peers, totals, top, bottom, received, messages, members))
+        kernel = functools.partial(receive_kernel, peers, [plans[p][0] for p in peers])
+        return result_call(kernel, [totals, top, bottom, *received], scans, members * ascans)
 
     def dense(received):
-        everyone = [("all", t) for t in range(TILES)]
-        message = ((0, rows + 8, rows, True),)
-        out = []
-        for part in (everyone[:half], everyone[half:]):
-            *some, _ = send(
-                part, spectra, tables, top, bottom, totals,
-                [message] * half, [(rows,) * members] * half,
-            )
-            out += some
-        swapped = lax.all_to_all(jnp.stack(out), "ascan", 0, 0, tiled=True)
-        pieces = [swapped[i] for i in range(members)]
-        return tuple(receive(everyone, totals, top, bottom, pieces, [message] * members, members))
+        out = dense_send(spectra, tables, top, bottom)
+        swapped = lax.all_to_all(out, "ascan", 0, 0, tiled=True)
+        return result_call(dense_receive_kernel, [totals, swapped], scans, members * ascans)
 
     outs = lax.cond(totals[2, 0] > 0.0, dense, quick, received)
     return (*outs, mean_flow)
+
+
+def flipped(length, bits):
+    return [(s, s ^ bits) for s in range(length)]
+
+
+def strides(length):
+    return [1 << bit for bit in range(length.bit_length() - 1)]
+
+
+def tile_groups(far, near, own):
+    return far[:1], far[1:2], far[2:], near + [own]
 
 
 def plain_body(spectra, surface_top, surface_bottom):

time: 99.8 us -> 94.6 us (0.948)
  starting transfers between devices: 53.2 us -> 44.1 us
  waiting for transfers between devices: 10.6 us -> 19.2 us
  Pallas kernels: 28.4 us -> 25.2 us
  local copies, waits for them, and re-layouts: 2.42 us -> 1.2 us
    ppermute x18 -> x15, starting transfers between devices: 40 us -> 28.8 us  [sparse_body(): message = lax.ppermute(message, 'ascan', pairs)]
    ppermute x18 -> x15, waiting for transfers between devices: 4.09 us -> 8.83 us  [sparse_body(): message = lax.ppermute(message, 'ascan', pairs)]
    ppermute x5 -> x6, waiting for transfers between devices: 6.53 us -> 10.4 us  [the longest x3 5.52 us: sparse_body(): shares.append(lax.ppermute(stats, 'ascan', flipped(members, bits)))]
    pallas_call x5, Pallas kernels: 28.4 us -> 25.2 us  [the longest x4 19.3 us: send(): pl.pallas_call(functools.partial(send_kernel, peers, messages, rooms, sta...]
    ppermute x5 -> x6, starting transfers between devices: 13.2 us -> 15.3 us  [the longest x3 9.54 us: sparse_body(): shares.append(lax.ppermute(stats, 'ascan', flipped(members, bits)))]
    unnamed x34 -> x26, local copies, waits for them, and re-layouts: 1.9 us -> 0.68 us
  transfers between devices with their start and end apart: 23 -> 21, of which waited for: 8 -> 8; matrix products, arithmetic and copies ran while one was open for 1% -> 1% of each run, Pallas kernels for 17% -> 14%
where the time goes in v1:
time: 94.6 us; the launch traced here: 94.3 us
  starting transfers between devices  44.1 us (47%)
  Pallas kernels  25.2 us (27%)
  waiting for transfers between devices  19.2 us (20%)
  between operations  4 us (4%)
  local copies, waits for them, and re-layouts  1.2 us (1%)
    ppermute x15, starting transfers between devices, sparse_body(): message = lax.ppermute(message, 'ascan', pairs)  28.8 us
    pallas_call x4, Pallas kernels, send(): pl.pallas_call(functools.partial(send_kernel, peers, messages, rooms, sta...  19.3 us
    ppermute x3, starting transfers between devices, sparse_body(): shares.append(lax.ppermute(stats, 'ascan', flipped(members, bits)))  9.54 us
    ppermute x15, waiting for transfers between devices, sparse_body(): message = lax.ppermute(message, 'ascan', pairs)  8.83 us
    pallas_call x1, Pallas kernels, result_call(): pl.pallas_call(kernel, out_shape=[shape] * MAPS, in_specs=[VMEM] * len(op...  5.88 us
    ppermute x3, starting transfers between devices, sparse_body(): stats = stats + lax.ppermute(stats, axis, pairs)  5.74 us
    ppermute x3, waiting for transfers between devices, sparse_body(): shares.append(lax.ppermute(stats, 'ascan', flipped(members, bits)))  5.52 us
    ppermute x3, waiting for transfers between devices, sparse_body(): stats = stats + lax.ppermute(stats, axis, pairs)  4.84 us
  transfers between devices with their start and end apart: 21, of which 8 were waited for; matrix products, arithmetic and copies ran while one was open for 1% of the time, Pallas kernels for 14%

profile of v1, /device:TPU:0, one launch (start us, length us, event | category | flops | bytes accessed | tf_op | source)
XLA Modules:
  0.0 94.3 jit_solution(16042632014044862830)
XLA Ops:
  0.6 0.0 copy-start.1
  0.7 0.0 copy-start.2
  0.7 5.7 %shard_map.75 = (f32[96,384]{1,0:T(8,128)S(1)}, f32[56,384]{1,0:T(8,128)S(1)}, f32[72,384]{1,0:T(8,128)S(1)}, f32[8,128]{1,0:T(8,128)S(1)}, bf16[2,4,128,2048]{3...) custom-call(bf16[2,4,128,2048]{3,2,1,0:T(8,128)(2,1)} %x_ref.1, bf16[8,512,256]{2,1,0:T(8,128)(2,1)} %constant.14.table_ref, ...), custom_call_target="tpu_custom_call" | custom-call | flops 1073741824 | bytes 4194304 | tf_op jit(solution)/shard_map/pallas_call | solution.py:325
  6.3 0.7 collective-permute-start.7
  7.0 0.0 copy-done.1
  7.0 0.0 copy-done.2
  7.0 2.2 %shard_map.76 = (f32[96,384]{1,0:T(8,128)S(1)}, f32[56,384]{1,0:T(8,128)S(1)}, f32[64,384]{1,0:T(8,128)S(1)}, f32[8,128]{1,0:T(8,128)S(1)}) custom-call(bf16[2,4,128,2048]{3,2,1,0:T(8,128)(2,1)S(1)} %get-tuple-element.101.x_ref, bf16[8,512,256]{2,1,0:T(8,128)(2,1)S(1)} %get-tuple-element.102.table_ref, s32[2,128]{1,0:T(2,128)S(1)} %copy-done.1, ...), custom_call_target="tpu_custom_call" | custom-call | flops 1073741824 | bytes 4194304 | tf_op jit(solution)/shard_map/pallas_call | solution.py:325
  9.2 0.7 collective-permute-start.10
  9.9 3.9 %shard_map.77 = (f32[96,384]{1,0:T(8,128)S(1)}, f32[56,384]{1,0:T(8,128)S(1)}, f32[56,384]{1,0:T(8,128)S(1)}, f32[96,384]{1,0:T(8,128)S(1)}, f32[56,384]{1,0:T(8...) custom-call(bf16[2,4,128,2048]{3,2,1,0:T(8,128)(2,1)S(1)} %get-tuple-element.101.x_ref, ...), custom_call_target="tpu_custom_call" | custom-call | flops 2147483648 | bytes 4194304 | tf_op jit(solution)/shard_map/pallas_call | solution.py:325
  13.8 0.8 collective-permute-start.17
  14.6 0.0 copy-start
  14.6 7.6 %shard_map.78 = (f32[184,384]{1,0:T(8,128)S(1)}, f32[184,384]{1,0:T(8,128)S(1)}, f32[184,384]{1,0:T(8,128)S(1)}, f32[256,384]{1,0:T(8,128)}, f32[8,128]{1,0:T(8,128)S(1)}) custom-call(bf16[2,4,128,2048]{3,2,1,0:T(8,128)(2,1)S(1)} %get-tuple-element.101.x_ref, bf16[8,512,256]{2,1,0:T(8,128)(2,1)S(1)} %get-tuple-element.102.table_ref, s32[2,128]{1,0:T(2,128)S(1)} %copy-done.1, ...), custom_call_target="tpu_custom_call" | custom-call | flops 4294967296 | bytes 4194304 | tf_op jit(solution)/shard_map/pallas_call | solution.py:325
  22.2 4.2 %collective-permute-start = (f32[8,128]{1,0:T(8,128)S(1)}, f32[8,128]{1,0:T(8,128)S(1)}, u32[]{:S(2)}, u32[]{:S(2)}) collective-permute-start(f32[8,128]{1,0:T(8,128)S(1)} %get-tuple-element.106), channel_id=1, source_target_pairs={{0,1},{1,0},{2,3},{3,2},{4,5},{5,4},{6,7},{7,6},{8,9},{9,8},{10,11... | collective-permute-start | bytes 12296 | tf_op jit(solution)/shard_map/ppermute | solution.py:538
  26.4 1.6 %collective-permute-done = f32[8,128]{1,0:T(8,128)S(1)} collective-permute-done((f32[8,128]{1,0:T(8,128)S(1)}, f32[8,128]{1,0:T(8,128)S(1)}, u32[]{:S(2)}, u32[]{:S(2)}) %collective-permute-start) | collective-permute-done | bytes 4128 | tf_op jit(solution)/shard_map/ppermute | solution.py:538
  28.0 0.0 collective-permute-start.1
  28.0 1.2 %collective-permute-done.1 = f32[8,128]{1,0:T(8,128)S(1)} collective-permute-done((f32[8,128]{1,0:T(8,128)S(1)}, f32[8,128]{1,0:T(8,128)S(1)}, u32[]{:S(2)}, u32[]{:S(2)}) %collective-permute-start.1) | collective-permute-done | bytes 4128 | tf_op jit(solution)/shard_map/ppermute | solution.py:538
  29.2 1.5 %collective-permute-start.2 = (f32[8,128]{1,0:T(8,128)S(1)}, f32[8,128]{1,0:T(8,128)S(1)}, u32[]{:S(2)}, u32[]{:S(2)}) collective-permute-start(f32[8,128]{1,0:T(8,128)S(1)} %add.19), channel_id=1, source_target_pairs={{0,16},{8,24},{16,0},{24,8},{1,17},{9,25},{17,1},{25,9},{2,18},{10... | collective-permute-start | bytes 12296 | tf_op jit(solution)/shard_map/ppermute | solution.py:538
  30.7 2.1 %collective-permute-done.2 = f32[8,128]{1,0:T(8,128)S(1)} collective-permute-done((f32[8,128]{1,0:T(8,128)S(1)}, f32[8,128]{1,0:T(8,128)S(1)}, u32[]{:S(2)}, u32[]{:S(2)}) %collective-permute-start.2) | collective-permute-done | bytes 4128 | tf_op jit(solution)/shard_map/ppermute | solution.py:538
  32.8 6.0 %collective-permute-start.5 = (f32[8,128]{1,0:T(8,128)S(1)}, f32[8,128]{1,0:T(8,128)S(1)}, u32[]{:S(2)}, u32[]{:S(2)}) collective-permute-start(f32[8,128]{1,0:T(8,128)S(1)} %add.20), channel_id=1, source_target_pairs={{0,6},{1,7},{2,4},{3,5},{4,2},{5,3},{6,0},{7,1},{8,14},{9,15},{10,... | collective-permute-start | bytes 12296 | tf_op jit(solution)/shard_map/ppermute | solution.py:547
  38.8 0.7 collective-permute-start.8
  39.5 0.9 collective-permute-done.5
  40.4 1.7 %collective-permute-start.4 = (f32[8,128]{1,0:T(8,128)S(1)}, f32[8,128]{1,0:T(8,128)S(1)}, u32[]{:S(2)}, u32[]{:S(2)}) collective-permute-start(f32[8,128]{1,0:T(8,128)S(1)} %add.20), channel_id=1, source_target_pairs={{0,4},{1,5},{2,6},{3,7},{4,0},{5,1},{6,2},{7,3},{8,12},{9,13},{10,... | collective-permute-start | bytes 12296 | tf_op jit(solution)/shard_map/ppermute | solution.py:547
  42.2 2.8 %collective-permute-done.4 = f32[8,128]{1,0:T(8,128)S(1)} collective-permute-done((f32[8,128]{1,0:T(8,128)S(1)}, f32[8,128]{1,0:T(8,128)S(1)}, u32[]{:S(2)}, u32[]{:S(2)}) %collective-permute-start.4) | collective-permute-done | bytes 4128 | tf_op jit(solution)/shard_map/ppermute | solution.py:547
  44.9 1.8 %collective-permute-start.3 = (f32[8,128]{1,0:T(8,128)S(1)}, f32[8,128]{1,0:T(8,128)S(1)}, u32[]{:S(2)}, u32[]{:S(2)}) collective-permute-start(f32[8,128]{1,0:T(8,128)S(1)} %add.20), channel_id=1, source_target_pairs={{0,2},{1,3},{2,0},{3,1},{4,6},{5,7},{6,4},{7,5},{8,10},{9,11},{10,... | collective-permute-start | bytes 12296 | tf_op jit(solution)/shard_map/ppermute | solution.py:547
  46.7 1.8 %collective-permute-done.3 = f32[8,128]{1,0:T(8,128)S(1)} collective-permute-done((f32[8,128]{1,0:T(8,128)S(1)}, f32[8,128]{1,0:T(8,128)S(1)}, u32[]{:S(2)}, u32[]{:S(2)}) %collective-permute-start.3) | collective-permute-done | bytes 4128 | tf_op jit(solution)/shard_map/ppermute | solution.py:547
  48.5 0.7 collective-permute-start.11
  49.2 0.0 collective-permute-done.17
  49.2 0.0 copy-start.12
  49.2 0.7 collective-permute-start.13
  49.9 0.0 collective-permute-done.7
  49.9 0.0 copy-start.7
  49.9 0.7 collective-permute-start.14
  50.6 0.0 collective-permute-done.10
  50.6 0.0 copy-start.8
  50.6 0.7 collective-permute-start.16
  51.3 0.0 collective-permute-done.13
  51.3 0.0 copy-start.9
  51.3 0.6 copy-done.9
  51.9 11.7 %collective-permute-start.6 = (f32[96,384]{1,0:T(8,128)S(1)}, f32[96,384]{1,0:T(8,128)S(1)}, u32[]{:S(2)}, u32[]{:S(2)}) collective-permute-start(f32[96,384]{1,0:T(8,128)S(1)} %get-tuple-element.107), channel_id=1, source_target_pairs={{0,4},{1,5},{2,6},{3,7},{4,0},{5,1},{6,2},{7,3},{8,12},{9,13},{10,... | collective-permute-start | bytes 442376 | tf_op jit(solution)/shard_map/ppermute | solution.py:544
  63.6 0.0 collective-permute-done.14
  63.6 3.3 %collective-permute-start.9 = (f32[96,384]{1,0:T(8,128)S(1)}, f32[96,384]{1,0:T(8,128)S(1)}, u32[]{:S(2)}, u32[]{:S(2)}) collective-permute-start(f32[96,384]{1,0:T(8,128)S(1)} %get-tuple-element.110), channel_id=1, source_target_pairs={{0,5},{1,6},{2,7},{3,4},{4,1},{5,2},{6,3},{7,0},{8,13},{9,14},{10,... | collective-permute-start | bytes 442376 | tf_op jit(solution)/shard_map/ppermute | solution.py:544
  66.9 0.0 collective-permute-done.16
  66.9 1.6 %collective-permute-start.18 = (f32[184,384]{1,0:T(8,128)S(1)}, f32[184,384]{1,0:T(8,128)S(1)}, u32[]{:S(2)}, u32[]{:S(2)}) collective-permute-start(f32[184,384]{1,0:T(8,128)S(1)} %get-tuple-element.119), channel_id=1, source_target_pairs={{0,1},{1,0},{2,3},{3,2},{4,5},{5,4},{6,7},{7,6},{8,9},{9,8},{10,11... | collective-permute-start | bytes 847880 | tf_op jit(solution)/shard_map/ppermute | solution.py:544
  68.5 0.0 collective-permute-done.11
  68.5 1.3 %collective-permute-start.19 = (f32[184,384]{1,0:T(8,128)S(1)}, f32[184,384]{1,0:T(8,128)}, u32[]{:S(2)}, u32[]{:S(2)}) collective-permute-start(f32[184,384]{1,0:T(8,128)S(1)} %get-tuple-element.120), channel_id=1, source_target_pairs={{0,2},{1,3},{2,0},{3,1},{4,6},{5,7},{6,4},{7,5},{8,10},{9,11},{10,... | collective-permute-start | bytes 847880 | tf_op jit(solution)/shard_map/ppermute | solution.py:544
  69.7 0.0 collective-permute-done.8
  69.7 1.5 %collective-permute-start.20 = (f32[184,384]{1,0:T(8,128)S(1)}, f32[184,384]{1,0:T(8,128)}, u32[]{:S(2)}, u32[]{:S(2)}) collective-permute-start(f32[184,384]{1,0:T(8,128)S(1)} %get-tuple-element.121), channel_id=1, source_target_pairs={{0,3},{1,2},{2,1},{3,0},{4,7},{5,6},{6,5},{7,4},{8,11},{9,10},{10,... | collective-permute-start | bytes 847880 | tf_op jit(solution)/shard_map/ppermute | solution.py:544
  71.2 5.4 %collective-permute-done.6 = f32[96,384]{1,0:T(8,128)S(1)} collective-permute-done((f32[96,384]{1,0:T(8,128)S(1)}, f32[96,384]{1,0:T(8,128)S(1)}, u32[]{:S(2)}, u32[]{:S(2)}) %collective-permute-start.6) | collective-permute-done | bytes 147488 | tf_op jit(solution)/shard_map/ppermute | solution.py:544
  76.6 0.0 collective-permute-start.12
  76.6 0.0 collective-permute-done.9
  76.6 0.0 copy-start.4
  76.6 4.0 %collective-permute-start.15 = (f32[96,384]{1,0:T(8,128)S(1)}, f32[96,384]{1,0:T(8,128)}, u32[]{:S(2)}, u32[]{:S(2)}) collective-permute-start(f32[96,384]{1,0:T(8,128)S(1)} %get-tuple-element.116), channel_id=1, source_target_pairs={{0,7},{1,4},{2,5},{3,6},{4,3},{5,0},{6,1},{7,2},{8,15},{9,12},{10,... | collective-permute-start | bytes 442376 | tf_op jit(solution)/shard_map/ppermute | solution.py:544
  80.7 0.0 copy-done.3
  80.7 0.5 fusion
  81.2 0.0 copy-done.4
  82.5 0.6 slice_reduce_fusion
  83.1 0.0 copy-done.12
  83.8 0.0 collective-permute-done.12
  83.8 3.4 %collective-permute-done.15 = f32[96,384]{1,0:T(8,128)} collective-permute-done((f32[96,384]{1,0:T(8,128)S(1)}, f32[96,384]{1,0:T(8,128)}, u32[]{:S(2)}, u32[]{:S(2)}) %collective-permute-start.15) | collective-permute-done | bytes 147488 | tf_op jit(solution)/shard_map/ppermute | solution.py:544
  87.2 0.0 collective-permute-done.18
  87.2 0.0 collective-permute-done.19
  87.2 0.0 collective-permute-done.20
  87.2 5.9 %conditional.1 = ((f32[2,128,1024]{2,1,0:T(8,128)}, f32[2,128,1024]{2,1,0:T(8,128)}, f32[2,128,1024]{2,1,0:T(8,128)})) conditional(s32[]{:T(128)} %bitcast, (f32[8,128]{1,0:T(8,128)S(1)}, s32[2,128]{1,0:T(2,128)S(1)}, s32[2,128]{1,0:T(2,128)S(1)}, f32[96,384]{1,0:T(8,128)}, f32[56,384]{1,0:T(8,128)}, /*index=5*/f32[72,384]{1,0:T(8,128)}, ...), branch_computations={%region_0.0_spmd, %region_1.0_spmd} | conditional | flops 805306368 | bytes 12582920 | solution.py:560
  87.2 5.9 %branch_0_fun.1 = (f32[2,128,1024]{2,1,0:T(8,128)}, f32[2,128,1024]{2,1,0:T(8,128)}, f32[2,128,1024]{2,1,0:T(8,128)}) custom-call(f32[8,128]{1,0:T(8,128)S(1)} %get-tuple-element.48.totals_ref, s32[2,128]{1,0:T(2,128)S(1)} %get-tuple-element.49.top_ref, s32[2,128]{1,0:T(2,128)S(1)} %get-tuple-element.50.bottom_ref, f32[96,384]{1,0:T(8,128)} %get-tuple-element.51.refs_0_, ...), custom_call_target="tpu_custom_call" | custom-call | flops 805306368 | bytes 6291456 | tf_op jit(solution)/shard_map/cond/branch_0_fun/pallas_call | solution.py:429
  (17 shorter events, 0.0 us)
Async XLA Ops:
  0.6 6.4 %copy-start.1 = (s32[2,128]{1,0:T(2,128)S(1)}, s32[2,128]{1,0:T(2,128)}, u32[]{:S(2)}) copy-start(s32[2,128]{1,0:T(2,128)} %top_ref.7) | copy-start | bytes 3076
  0.7 6.4 %copy-start.2 = (s32[2,128]{1,0:T(2,128)S(1)}, s32[2,128]{1,0:T(2,128)}, u32[]{:S(2)}) copy-start(s32[2,128]{1,0:T(2,128)} %bottom_ref.7) | copy-start | bytes 3076
  6.3 43.6 %collective-permute-start.7 = (f32[56,384]{1,0:T(8,128)S(1)}, f32[56,384]{1,0:T(8,128)S(1)}, u32[]{:S(2)}, u32[]{:S(2)}) collective-permute-start(f32[56,384]{1,0:T(8,128)S(1)} %get-tuple-element.108), channel_id=1, source_target_pairs={{5,1},{6,2},{7,3},{13,9},{14,10},{15,11},{21,17},{22,18},{23,19},{... | collective-permute-start | bytes 258056 | tf_op jit(solution)/shard_map/ppermute | solution.py:544
  9.2 41.4 %collective-permute-start.10 = (f32[56,384]{1,0:T(8,128)S(1)}, f32[56,384]{1,0:T(8,128)S(1)}, u32[]{:S(2)}, u32[]{:S(2)}) collective-permute-start(f32[56,384]{1,0:T(8,128)S(1)} %get-tuple-element.111), channel_id=1, source_target_pairs={{4,1},{5,2},{6,3},{12,9},{13,10},{14,11},{20,17},{21,18},{22,19},{... | collective-permute-start | bytes 258056 | tf_op jit(solution)/shard_map/ppermute | solution.py:544
  13.8 35.4 %collective-permute-start.17 = (f32[48,384]{1,0:T(8,128)S(1)}, f32[48,384]{1,0:T(8,128)S(1)}, u32[]{:S(2)}, u32[]{:S(2)}) collective-permute-start(f32[48,384]{1,0:T(8,128)S(1)} %get-tuple-element.118), channel_id=1, source_target_pairs={{4,3},{7,2},{12,11},{15,10},{20,19},{23,18},{28,27},{31,26}} | collective-permute-start | bytes 221192 | tf_op jit(solution)/shard_map/ppermute | solution.py:544
  14.6 72.6 %copy-start = (bf16[8,512,256]{2,1,0:T(8,128)(2,1)S(1)}, bf16[8,512,256]{2,1,0:T(8,128)(2,1)}, u32[]{:S(2)}) copy-start(bf16[8,512,256]{2,1,0:T(8,128)(2,1)} %constant.14.table_ref) | copy-start | bytes 6291460
  22.2 5.8 %collective-permute-start = (f32[8,128]{1,0:T(8,128)S(1)}, f32[8,128]{1,0:T(8,128)S(1)}, u32[]{:S(2)}, u32[]{:S(2)}) collective-permute-start(f32[8,128]{1,0:T(8,128)S(1)} %get-tuple-element.106), channel_id=1, source_target_pairs={{0,1},{1,0},{2,3},{3,2},{4,5},{5,4},{6,7},{7,6},{8,9},{9,8},{10,11... | collective-permute-start | bytes 12296 | tf_op jit(solution)/shard_map/ppermute | solution.py:538
  28.0 1.2 %collective-permute-start.1 = (f32[8,128]{1,0:T(8,128)S(1)}, f32[8,128]{1,0:T(8,128)S(1)}, u32[]{:S(2)}, u32[]{:S(2)}) collective-permute-start(f32[8,128]{1,0:T(8,128)S(1)} %add.18), channel_id=1, source_target_pairs={{0,8},{8,0},{16,24},{24,16},{1,9},{9,1},{17,25},{25,17},{2,10},{10... | collective-permute-start | bytes 12296 | tf_op jit(solution)/shard_map/ppermute | solution.py:538
  29.2 3.6 %collective-permute-start.2 = (f32[8,128]{1,0:T(8,128)S(1)}, f32[8,128]{1,0:T(8,128)S(1)}, u32[]{:S(2)}, u32[]{:S(2)}) collective-permute-start(f32[8,128]{1,0:T(8,128)S(1)} %add.19), channel_id=1, source_target_pairs={{0,16},{8,24},{16,0},{24,8},{1,17},{9,25},{17,1},{25,9},{2,18},{10... | collective-permute-start | bytes 12296 | tf_op jit(solution)/shard_map/ppermute | solution.py:538
  32.8 7.6 %collective-permute-start.5 = (f32[8,128]{1,0:T(8,128)S(1)}, f32[8,128]{1,0:T(8,128)S(1)}, u32[]{:S(2)}, u32[]{:S(2)}) collective-permute-start(f32[8,128]{1,0:T(8,128)S(1)} %add.20), channel_id=1, source_target_pairs={{0,6},{1,7},{2,4},{3,5},{4,2},{5,3},{6,0},{7,1},{8,14},{9,15},{10,... | collective-permute-start | bytes 12296 | tf_op jit(solution)/shard_map/ppermute | solution.py:547
  38.8 30.9 %collective-permute-start.8 = (f32[72,384]{1,0:T(8,128)S(1)}, f32[72,384]{1,0:T(8,128)S(1)}, u32[]{:S(2)}, u32[]{:S(2)}) collective-permute-start(f32[72,384]{1,0:T(8,128)S(1)} %get-tuple-element.109), channel_id=1, source_target_pairs={{6,2},{7,3},{14,10},{15,11},{22,18},{23,19},{30,26},{31,27}} | collective-permute-start | bytes 331784 | tf_op jit(solution)/shard_map/ppermute | solution.py:544
  40.4 4.5 %collective-permute-start.4 = (f32[8,128]{1,0:T(8,128)S(1)}, f32[8,128]{1,0:T(8,128)S(1)}, u32[]{:S(2)}, u32[]{:S(2)}) collective-permute-start(f32[8,128]{1,0:T(8,128)S(1)} %add.20), channel_id=1, source_target_pairs={{0,4},{1,5},{2,6},{3,7},{4,0},{5,1},{6,2},{7,3},{8,12},{9,13},{10,... | collective-permute-start | bytes 12296 | tf_op jit(solution)/shard_map/ppermute | solution.py:547
  44.9 3.6 %collective-permute-start.3 = (f32[8,128]{1,0:T(8,128)S(1)}, f32[8,128]{1,0:T(8,128)S(1)}, u32[]{:S(2)}, u32[]{:S(2)}) collective-permute-start(f32[8,128]{1,0:T(8,128)S(1)} %add.20), channel_id=1, source_target_pairs={{0,2},{1,3},{2,0},{3,1},{4,6},{5,7},{6,4},{7,5},{8,10},{9,11},{10,... | collective-permute-start | bytes 12296 | tf_op jit(solution)/shard_map/ppermute | solution.py:547
  48.5 19.9 %collective-permute-start.11 = (f32[64,384]{1,0:T(8,128)S(1)}, f32[64,384]{1,0:T(8,128)S(1)}, u32[]{:S(2)}, u32[]{:S(2)}) collective-permute-start(f32[64,384]{1,0:T(8,128)S(1)} %get-tuple-element.112), channel_id=1, source_target_pairs={{5,2},{6,3},{13,10},{14,11},{21,18},{22,19},{29,26},{30,27}} | collective-permute-start | bytes 294920 | tf_op jit(solution)/shard_map/ppermute | solution.py:544
  49.2 33.9 %copy-start.12 = (f32[48,384]{1,0:T(8,128)}, f32[48,384]{1,0:T(8,128)S(1)}, u32[]{:S(2)}) copy-start(f32[48,384]{1,0:T(8,128)S(1)} %collective-permute-done.17) | copy-start | bytes 221188
  49.2 2.1 %collective-permute-start.13 = (f32[56,384]{1,0:T(8,128)S(1)}, f32[56,384]{1,0:T(8,128)S(1)}, u32[]{:S(2)}, u32[]{:S(2)}) collective-permute-start(f32[56,384]{1,0:T(8,128)S(1)} %get-tuple-element.114), channel_id=1, source_target_pairs={{4,2},{5,3},{7,1},{12,10},{13,11},{15,9},{20,18},{21,19},{23,17},{... | collective-permute-start | bytes 258056 | tf_op jit(solution)/shard_map/ppermute | solution.py:544
  49.9 31.9 %copy-start.7 = (f32[56,384]{1,0:T(8,128)}, f32[56,384]{1,0:T(8,128)S(1)}, u32[]{:S(2)}) copy-start(f32[56,384]{1,0:T(8,128)S(1)} %collective-permute-done.7) | copy-start | bytes 258052
  49.9 13.7 %collective-permute-start.14 = (f32[56,384]{1,0:T(8,128)S(1)}, f32[56,384]{1,0:T(8,128)S(1)}, u32[]{:S(2)}, u32[]{:S(2)}) collective-permute-start(f32[56,384]{1,0:T(8,128)S(1)} %get-tuple-element.115), channel_id=1, source_target_pairs={{4,2},{5,3},{12,10},{13,11},{20,18},{21,19},{28,26},{29,27}} | collective-permute-start | bytes 258056 | tf_op jit(solution)/shard_map/ppermute | solution.py:544
  50.6 31.3 %copy-start.8 = (f32[56,384]{1,0:T(8,128)}, f32[56,384]{1,0:T(8,128)S(1)}, u32[]{:S(2)}) copy-start(f32[56,384]{1,0:T(8,128)S(1)} %collective-permute-done.10) | copy-start | bytes 258052
  50.6 16.3 %collective-permute-start.16 = (f32[56,384]{1,0:T(8,128)S(1)}, f32[56,384]{1,0:T(8,128)S(1)}, u32[]{:S(2)}, u32[]{:S(2)}) collective-permute-start(f32[56,384]{1,0:T(8,128)S(1)} %get-tuple-element.117), channel_id=1, source_target_pairs={{4,3},{6,1},{7,2},{12,11},{14,9},{15,10},{20,19},{22,17},{23,18},{... | collective-permute-start | bytes 258056 | tf_op jit(solution)/shard_map/ppermute | solution.py:544
  51.3 0.6 copy-start.9
  51.9 24.7 %collective-permute-start.6 = (f32[96,384]{1,0:T(8,128)S(1)}, f32[96,384]{1,0:T(8,128)S(1)}, u32[]{:S(2)}, u32[]{:S(2)}) collective-permute-start(f32[96,384]{1,0:T(8,128)S(1)} %get-tuple-element.107), channel_id=1, source_target_pairs={{0,4},{1,5},{2,6},{3,7},{4,0},{5,1},{6,2},{7,3},{8,12},{9,13},{10,... | collective-permute-start | bytes 442376 | tf_op jit(solution)/shard_map/ppermute | solution.py:544
  63.6 18.3 %copy-start.10 = (f32[56,384]{1,0:T(8,128)}, f32[56,384]{1,0:T(8,128)S(1)}, u32[]{:S(2)}) copy-start(f32[56,384]{1,0:T(8,128)S(1)} %collective-permute-done.14) | copy-start | bytes 258052
  63.6 13.0 %collective-permute-start.9 = (f32[96,384]{1,0:T(8,128)S(1)}, f32[96,384]{1,0:T(8,128)S(1)}, u32[]{:S(2)}, u32[]{:S(2)}) collective-permute-start(f32[96,384]{1,0:T(8,128)S(1)} %get-tuple-element.110), channel_id=1, source_target_pairs={{0,5},{1,6},{2,7},{3,4},{4,1},{5,2},{6,3},{7,0},{8,13},{9,14},{10,... | collective-permute-start | bytes 442376 | tf_op jit(solution)/shard_map/ppermute | solution.py:544
  66.9 15.6 %copy-start.11 = (f32[56,384]{1,0:T(8,128)}, f32[56,384]{1,0:T(8,128)S(1)}, u32[]{:S(2)}) copy-start(f32[56,384]{1,0:T(8,128)S(1)} %collective-permute-done.16) | copy-start | bytes 258052
  66.9 20.3 %collective-permute-start.18 = (f32[184,384]{1,0:T(8,128)S(1)}, f32[184,384]{1,0:T(8,128)S(1)}, u32[]{:S(2)}, u32[]{:S(2)}) collective-permute-start(f32[184,384]{1,0:T(8,128)S(1)} %get-tuple-element.119), channel_id=1, source_target_pairs={{0,1},{1,0},{2,3},{3,2},{4,5},{5,4},{6,7},{7,6},{8,9},{9,8},{10,11... | collective-permute-start | bytes 847880 | tf_op jit(solution)/shard_map/ppermute | solution.py:544
  68.5 12.7 %copy-start.6 = (f32[64,384]{1,0:T(8,128)}, f32[64,384]{1,0:T(8,128)S(1)}, u32[]{:S(2)}) copy-start(f32[64,384]{1,0:T(8,128)S(1)} %collective-permute-done.11) | copy-start | bytes 294916
  68.5 18.7 %collective-permute-start.19 = (f32[184,384]{1,0:T(8,128)S(1)}, f32[184,384]{1,0:T(8,128)}, u32[]{:S(2)}, u32[]{:S(2)}) collective-permute-start(f32[184,384]{1,0:T(8,128)S(1)} %get-tuple-element.120), channel_id=1, source_target_pairs={{0,2},{1,3},{2,0},{3,1},{4,6},{5,7},{6,4},{7,5},{8,10},{9,11},{10,... | collective-permute-start | bytes 847880 | tf_op jit(solution)/shard_map/ppermute | solution.py:544
  69.7 11.5 %copy-start.5 = (f32[72,384]{1,0:T(8,128)}, f32[72,384]{1,0:T(8,128)S(1)}, u32[]{:S(2)}) copy-start(f32[72,384]{1,0:T(8,128)S(1)} %collective-permute-done.8) | copy-start | bytes 331780
  69.7 17.5 %collective-permute-start.20 = (f32[184,384]{1,0:T(8,128)S(1)}, f32[184,384]{1,0:T(8,128)}, u32[]{:S(2)}, u32[]{:S(2)}) collective-permute-start(f32[184,384]{1,0:T(8,128)S(1)} %get-tuple-element.121), channel_id=1, source_target_pairs={{0,3},{1,2},{2,1},{3,0},{4,7},{5,6},{6,5},{7,4},{8,11},{9,10},{10,... | collective-permute-start | bytes 847880 | tf_op jit(solution)/shard_map/ppermute | solution.py:544
  76.6 4.1 %copy-start.3 = (f32[96,384]{1,0:T(8,128)}, f32[96,384]{1,0:T(8,128)S(1)}, u32[]{:S(2)}) copy-start(f32[96,384]{1,0:T(8,128)S(1)} %collective-permute-done.6) | copy-start | bytes 442372
  76.6 7.2 %collective-permute-start.12 = (f32[96,384]{1,0:T(8,128)S(1)}, f32[96,384]{1,0:T(8,128)}, u32[]{:S(2)}, u32[]{:S(2)}) collective-permute-start(f32[96,384]{1,0:T(8,128)S(1)} %get-tuple-element.113), channel_id=1, source_target_pairs={{0,6},{1,7},{2,4},{3,5},{4,2},{5,3},{6,0},{7,1},{8,14},{9,15},{10,... | collective-permute-start | bytes 442376 | tf_op jit(solution)/shard_map/ppermute | solution.py:544
  76.6 4.6 %copy-start.4 = (f32[96,384]{1,0:T(8,128)}, f32[96,384]{1,0:T(8,128)S(1)}, u32[]{:S(2)}) copy-start(f32[96,384]{1,0:T(8,128)S(1)} %collective-permute-done.9) | copy-start | bytes 442372
  76.6 10.6 %collective-permute-start.15 = (f32[96,384]{1,0:T(8,128)S(1)}, f32[96,384]{1,0:T(8,128)}, u32[]{:S(2)}, u32[]{:S(2)}) collective-permute-start(f32[96,384]{1,0:T(8,128)S(1)} %get-tuple-element.116), channel_id=1, source_target_pairs={{0,7},{1,4},{2,5},{3,6},{4,3},{5,0},{6,1},{7,2},{8,15},{9,12},{10,... | collective-permute-start | bytes 442376 | tf_op jit(solution)/shard_map/ppermute | solution.py:544

commit v2 on v1

--- a/solution.py
+++ b/solution.py
@@ -21,7 +21,6 @@
 VARIANCE_SCALE = 0.1
 HEAD = 2
 MERGE = 44
-UNROLL = 4
 MAPS = 3
 
 
@@ -126,13 +125,11 @@
     return me ^ index if kind == "near" else index
 
 
-def send_kernel(peers, messages, rooms, staged, x_ref, table_ref, top_ref, bottom_ref, stats_in, *refs):
+def send_kernel(peers, messages, x_ref, table_ref, top_ref, bottom_ref, stats_in, *refs):
     count = sum(len(m) for m in messages)
     outs = refs[:count]
     stats_ref, *rest = refs[count:]
-    if staged:
-        x_vmem, table_vmem, *rest = rest
-    profile_ref, maps_ref, *rest = rest
+    profile_ref, maps_ref = rest
     slots = len(peers)
     scans, _, ascans, _ = x_ref.shape
     me = lax.axis_index("ascan")
@@ -142,78 +139,56 @@
     def lanes_of(band):
         return slice(band * BAND_BINS, (band + 1) * BAND_BINS)
 
-    if staged:
-        x_sem, table_sem = rest
-
-        def x_copy(scan):
-            return pltpu.make_async_copy(x_ref.at[scan], x_vmem.at[scan], x_sem.at[scan])
-
-        first = tiles[0]
-
-        def table_copy(index):
-            tile = (first + index) & (TILES - 1)
-            return pltpu.make_async_copy(
-                table_ref.at[tile], table_vmem.at[tile], table_sem.at[index]
-            )
-
-        table_copy(0).start()
-        for scan in range(scans):
-            x_copy(scan).start()
-        for index in range(1, TILES):
-            table_copy(index).start()
-        x_used, table_used = x_vmem, table_vmem
-    else:
-        x_used, table_used = x_ref, table_ref
-
-    def product(weights, slot, scan, buf, band):
-        if staged and slot == 0 and band == 0:
-            x_copy(scan).wait()
-        x = x_used[scan, :, :, lanes_of(band)].reshape(REPEATS * ascans, BAND_BINS)
+    def product(weights, scan, buf, band):
+        x = x_ref[scan, :, :, lanes_of(band)].reshape(REPEATS * ascans, BAND_BINS)
         profile_ref[buf, band] = jnp.dot(x, weights, preferred_element_type=jnp.float32)
 
     def weights_of(slot):
-        chosen = tiles[0]
-        for i in range(1, slots):
-            chosen = jnp.where(slot == i, tiles[i], chosen)
-        return table_used[chosen]
+        return table_ref[tiles[slot]]
 
     def both(following, current):
         if following:
-            if staged and following == (0, 0):
-                table_copy(0).wait()
             weights = weights_of(following[0])
         share = ascans // BANDS
         for band in range(BANDS):
             if following:
-                product(weights, following[0], following[1], following[1] % 2, band)
+                product(weights, following[1], following[1] % 2, band)
             if current:
                 moments_rows(
                     profile_ref, current[1] % 2, maps_ref, *current, ascans, band * share, (band + 1) * share
                 )
 
-    if slots <= UNROLL:
+    top = flat_rows(top_ref[...])
+    bottom = flat_rows(bottom_ref[...])
+    rows = top.shape[1]
+    full = [
+        jnp.sum(jnp.where((top <= tile) & (tile < bottom), 1.0, 0.0)) > 0.0 for tile in tiles
+    ]
+    every = functools.reduce(jnp.logical_and, full)
+
+    @pl.when(every)
+    def _():
         order = [(slot, scan) for slot in range(slots) for scan in range(scans)]
         for following, current in zip(order + [None], [None] + order):
             both(following, current)
-    else:
-        both((0, 0), None)
-
-        def step(slot, carry):
-            for scan in range(scans - 1):
-                both((slot, scan + 1), (slot, scan))
-            both((jnp.minimum(slot + 1, slots - 1), 0), (slot, scans - 1))
-            return carry
-
-        lax.fori_loop(0, slots, step, 0)
-
-    if staged:
-        for index in range(1, TILES):
-            table_copy(index).wait()
-    top = flat_rows(top_ref[...])
-    bottom = flat_rows(bottom_ref[...])
-    rows = top.shape[1]
+
+    for slot in range(slots):
+
+        @pl.when(jnp.logical_not(full[slot]))
+        def _():
+            maps_ref[slot] = jnp.zeros(maps_ref.shape[1:], jnp.float32)
+
+        if slots > 1:
+
+            @pl.when(full[slot] & jnp.logical_not(every))
+            def _():
+                both((slot, 0), None)
+                for scan in range(scans - 1):
+                    both((slot, scan + 1), (slot, scan))
+                both(None, (slot, scans - 1))
+
     flow = jnp.zeros((8, TILE), jnp.float32)
-    held = over = jnp.float32(0.0)
+    held = jnp.float32(0.0)
     position = 0
     for slot, parts in enumerate(messages):
         mask, rank = tissue(top, bottom, tiles[slot])
@@ -223,10 +198,6 @@
         flow += jnp.dot(spread, low[:, :TILE], preferred_element_type=jnp.float32)
         count = jnp.sum(mask)
         held += count
-        room = jnp.float32(rows)
-        for source, value in enumerate(rooms[slot]):
-            room = jnp.where(me == source, jnp.float32(value), room)
-        over = jnp.where(count > room, 1.0, over)
         for first, size, carried, header in parts:
             out = outs[position]
             position += 1
@@ -239,7 +210,7 @@
                 out[carried + 1 : carried + 2, 0:rows] = bottom.astype(jnp.float32)
     line = lax.broadcasted_iota(jnp.int32, (8, TILE), 0)
     stats_ref[...] = stats_in[...] + jnp.where(
-        line == 0, flow, jnp.where(line == 1, held, jnp.where(line == 2, over, 0.0))
+        line == 0, flow, jnp.where(line == 1, held, 0.0)
     )
 
 
@@ -292,12 +263,12 @@
             pltpu.VMEM((1, BANDS, repeats * ascans, 2 * TILE), jnp.float32),
             pltpu.VMEM((1, rows, MAPS * TILE), jnp.float32),
         ],
-        compiler_params=pltpu.CompilerParams(vmem_limit_bytes=32 * 1024 * 1024),
+        compiler_params=pltpu.CompilerParams(vmem_limit_bytes=20 * 1024 * 1024),
         name="dense_send",
     )(spectra, tables, top, bottom)
 
 
-def send(peers, spectra, tables, top, bottom, stats, messages, rooms, staged=False):
+def send(peers, spectra, tables, top, bottom, stats, messages):
     scans, repeats, ascans, bins = spectra.shape
     assert scans % 2 == 0
     rows = scans * ascans
@@ -307,23 +278,13 @@
         for _, size, _, _ in parts
     ]
     shapes.append(jax.ShapeDtypeStruct((8, TILE), jnp.float32))
-    if staged:
-        assert len(peers) == 1
-        shapes.append(jax.ShapeDtypeStruct(spectra.shape, spectra.dtype))
-        shapes.append(jax.ShapeDtypeStruct(tables.shape, tables.dtype))
     scratch = [
         pltpu.VMEM((2, BANDS, repeats * ascans, 2 * TILE), jnp.float32),
         pltpu.VMEM((len(peers), rows, MAPS * TILE), jnp.float32),
     ]
     specs = [VMEM] * 5
-    if staged:
-        scratch += [
-            pltpu.SemaphoreType.DMA((scans,)),
-            pltpu.SemaphoreType.DMA((TILES,)),
-        ]
-        specs[:2] = [pl.BlockSpec(memory_space=pltpu.HBM)] * 2
     return pl.pallas_call(
-        functools.partial(send_kernel, peers, messages, rooms, staged),
+        functools.partial(send_kernel, peers, messages),
         out_shape=shapes,
         in_specs=specs,
         out_specs=[VMEM] * len(shapes),
@@ -337,9 +298,12 @@
     )(spectra, tables, top, bottom, stats)
 
 
-def mean_scale(totals):
-    flow = jnp.sum(totals[0:1, :], axis=1, keepdims=True)
-    return (totals[1:2, 0:1] * TILE) / (3.0 * flow)
+def mean_of(shares):
+    values = [share[...] for share in shares]
+    while len(values) > 1:
+        values = [a + b for a, b in zip(values[::2], values[1::2])]
+    flow = jnp.sum(values[0][0:1, :], axis=1, keepdims=True)
+    return flow / (values[0][1:2, 0:1] * TILE)
 
 
 def smooth(decorrelation_ref, angiogram_ref, scale):
@@ -351,7 +315,8 @@
             lane = lax.broadcasted_iota(jnp.int32, d.shape, 1)
             left = jnp.where(lane == 0, 0.0, pltpu.roll(d, 1, 1))
             right = jnp.where(lane == total - 1, 0.0, pltpu.roll(d, total - 1, 1))
-            angiogram_ref[scan, start : start + step, :] = ((left + d) + right) * scale
+            added = (left + d) + right
+            angiogram_ref[scan, start : start + step, :] = added if scale is None else added * scale
 
 
 def place(piece, choice):
@@ -364,7 +329,7 @@
     return result
 
 
-def receive_kernel(peers, messages, totals_ref, top_ref, bottom_ref, *refs):
+def receive_kernel(peers, messages, top_ref, bottom_ref, *refs):
     count = sum(len(m) for m in messages)
     ins = refs[:count]
     angiogram_ref, structure_ref, speckle_ref, decorrelation_ref = refs[count:]
@@ -397,10 +362,63 @@
             decorrelation_ref[scan, :, lanes] = result[0:TILE, columns]
             structure_ref[scan, :, lanes] = result[TILE : 2 * TILE, columns]
             speckle_ref[scan, :, lanes] = result[2 * TILE :, columns]
-    smooth(decorrelation_ref, angiogram_ref, mean_scale(totals_ref[...]))
-
-
-def dense_receive_kernel(totals_ref, pieces_ref, angiogram_ref, structure_ref, speckle_ref, decorrelation_ref):
+    smooth(decorrelation_ref, angiogram_ref, None)
+
+
+def finish_kernel(count, sums_ref, *refs):
+    shares, (angiogram_ref, mean_ref) = refs[:count], refs[count:]
+    mean = mean_of(shares)
+    mean_ref[...] = jnp.broadcast_to(mean, mean_ref.shape)
+    angiogram_ref[...] = sums_ref[...] * (1.0 / (3.0 * mean))
+
+
+def finish(sums, shares):
+    return pl.pallas_call(
+        functools.partial(finish_kernel, len(shares)),
+        out_shape=[
+            jax.ShapeDtypeStruct(sums.shape, jnp.float32),
+            jax.ShapeDtypeStruct((8, TILE), jnp.float32),
+        ],
+        in_specs=[VMEM] * (1 + len(shares)),
+        out_specs=[VMEM, VMEM],
+        compiler_params=pltpu.CompilerParams(vmem_limit_bytes=8 * 1024 * 1024),
+        name="finish_angiogram",
+    )(sums, *shares)
+
+
+def judge_kernel(peers, carried, room_ref, top_ref, bottom_ref, *refs):
+    pieces, out_ref = refs[:-1], refs[-1]
+    me = lax.axis_index("ascan")
+    half = lax.axis_size("ascan") // 2
+    own_top = flat_rows(top_ref[...]).astype(jnp.float32)
+    own_bottom = flat_rows(bottom_ref[...]).astype(jnp.float32)
+    rows = own_top.shape[1]
+    tile = lax.broadcasted_iota(jnp.int32, (TILES, rows), 0).astype(jnp.float32)
+    worst = jnp.full((TILES, 1), -1.0, jnp.float32)
+    surfaces = [(me, own_top, own_bottom)]
+    for peer, piece, line in zip(peers, pieces, carried):
+        origin = jnp.asarray(peer_origin(peer, me, half), jnp.int32)
+        surfaces.append((origin, piece[line : line + 1, 0:rows], piece[line + 1 : line + 2, 0:rows]))
+    for source, top, bottom in surfaces:
+        need = jnp.sum(jnp.where((top <= tile) & (tile < bottom), 1.0, 0.0), axis=1, keepdims=True)
+        worst = jnp.maximum(worst, need - room_ref[source][:, 0:1])
+    out_ref[0, 0] = jnp.where(jnp.max(worst) > 0.0, 1, 0).astype(jnp.int32)
+
+
+def judge(peers, carried, room, top, bottom, pieces):
+    return pl.pallas_call(
+        functools.partial(judge_kernel, peers, carried),
+        out_shape=jax.ShapeDtypeStruct((1, 1), jnp.int32),
+        in_specs=[VMEM] * (3 + len(pieces)),
+        out_specs=pl.BlockSpec(memory_space=pltpu.SMEM),
+        compiler_params=pltpu.CompilerParams(vmem_limit_bytes=8 * 1024 * 1024),
+        name="judge_room",
+    )(room, top, bottom, *pieces)
+
+
+def dense_receive_kernel(pieces_ref, *refs):
+    shares = refs[:-5]
+    angiogram_ref, structure_ref, speckle_ref, mean_ref, decorrelation_ref = refs[-5:]
     members, rows, _ = pieces_ref.shape
     scans = angiogram_ref.shape[0]
     ascans = rows // scans
@@ -420,24 +438,26 @@
         return carry
 
     lax.fori_loop(0, members, step, 0)
-    smooth(decorrelation_ref, angiogram_ref, mean_scale(totals_ref[...]))
-
-
-def result_call(kernel, operands, scans, total):
+    mean = mean_of(shares)
+    mean_ref[...] = jnp.broadcast_to(mean, mean_ref.shape)
+    smooth(decorrelation_ref, angiogram_ref, 1.0 / (3.0 * mean))
+
+
+def result_call(kernel, operands, scans, total, extra=()):
     shape = jax.ShapeDtypeStruct((scans, TILE, total), jnp.float32)
     return tuple(
         pl.pallas_call(
             kernel,
-            out_shape=[shape] * MAPS,
+            out_shape=[shape] * MAPS + list(extra),
             in_specs=[VMEM] * len(operands),
-            out_specs=[VMEM] * MAPS,
+            out_specs=[VMEM] * (MAPS + len(extra)),
             scratch_shapes=[pltpu.VMEM(shape.shape, jnp.float32)],
             cost_estimate=pl.CostEstimate(
                 flops=1024 * scans * MAPS * TILE * total,
                 bytes_accessed=8 * MAPS * scans * TILE * total,
                 transcendentals=0,
             ),
-            compiler_params=pltpu.CompilerParams(vmem_limit_bytes=24 * 1024 * 1024),
+            compiler_params=pltpu.CompilerParams(vmem_limit_bytes=16 * 1024 * 1024),
         )(*operands)
     )
 
@@ -505,32 +525,18 @@
 
 def sparse_body(members, spectra, top, bottom):
     scans, _, ascans, _ = spectra.shape
+    half = members // 2
     tables = tile_tables(TILE)
     plans, far, near, own = exchange_plans(members, scans, ascans)
     stats = jnp.zeros((8, TILE), jnp.float32)
     sent = {}
-    spectra_here, tables_here = spectra, tables
     peers = far + near + [own]
-    for number, group in enumerate(tile_groups(far, near, own)):
-        out = list(
-            send(
-                group,
-                spectra_here,
-                tables_here,
-                top,
-                bottom,
-                stats,
-                [plans[p][0] for p in group],
-                [plans[p][2] for p in group],
-                staged=number == 0,
-            )
-        )
+    for group in tile_groups(far, near, own):
+        out = list(send(group, spectra, tables, top, bottom, stats, [plans[p][0] for p in group]))
         for peer in group:
             for level in range(len(plans[peer][0])):
                 sent[peer, level] = out.pop(0)
         stats = out.pop(0)
-        if number == 0:
-            spectra_here, tables_here = out
     length = lax.axis_size("scan")
     hops = [("ascan", flipped(members, 1))]
     hops += [("scan", flipped(length, stride)) for stride in strides(length)]
@@ -545,19 +551,41 @@
             received.append(message)
     for bits in range(2, members, 2):
         shares.append(lax.ppermute(stats, "ascan", flipped(members, bits)))
-    totals = functools.reduce(jnp.add, shares)
-    mean_flow = jnp.sum(totals[0]) / (totals[1, 0] * TILE)
-
-    def quick(received):
-        kernel = functools.partial(receive_kernel, peers, [plans[p][0] for p in peers])
-        return result_call(kernel, [totals, top, bottom, *received], scans, members * ascans)
-
-    def dense(received):
+    heads = [peers.index(p) for p in far + near]
+    starts = np.cumsum([0] + [len(plans[p][0]) for p in peers])
+    room = np.zeros((members, TILES, 1), np.float32)
+    for peer in peers:
+        for source in range(members):
+            room[source, int(peer_target(peer, source, half)), 0] = plans[peer][2][source]
+    over = judge(
+        far + near,
+        [plans[p][0][0][2] for p in far + near],
+        jnp.asarray(np.broadcast_to(room, (members, TILES, TILE))),
+        top,
+        bottom,
+        [received[starts[i]] for i in heads],
+    )
+
+    kernel = functools.partial(receive_kernel, peers, [plans[p][0] for p in peers])
+    maps = result_call(kernel, [top, bottom, *received], scans, members * ascans)
+
+    def quick(maps):
+        angiogram, mean = finish(maps[0], shares)
+        return angiogram, maps[1], maps[2], mean
+
+    def dense(maps):
         out = dense_send(spectra, tables, top, bottom)
         swapped = lax.all_to_all(out, "ascan", 0, 0, tiled=True)
-        return result_call(dense_receive_kernel, [totals, swapped], scans, members * ascans)
-
-    outs = lax.cond(totals[2, 0] > 0.0, dense, quick, received)
+        return result_call(
+            dense_receive_kernel,
+            [swapped, *shares],
+            scans,
+            members * ascans,
+            [jax.ShapeDtypeStruct((8, TILE), jnp.float32)],
+        )
+
+    *outs, mean = lax.cond(over[0, 0] > 0, dense, quick, maps)
+    mean_flow = mean[0, 0]
     return (*outs, mean_flow)
 
 

time: 94.6 us -> 91.4 us (0.966)
  the two profiles are of different devices: /device:TPU:0 before, /device:TPU:2 now
where the time goes in v2:
time: 91.4 us; the launch traced here: 91.2 us
  waiting for transfers between devices  40.7 us (45%)
  starting transfers between devices  28.4 us (31%)
  Pallas kernels  19.9 us (22%)
  between operations  1.52 us (2%)
    ppermute x15, waiting for transfers between devices, sparse_body(): message = lax.ppermute(message, 'ascan', pairs)  25.1 us
    ppermute x15, starting transfers between devices, sparse_body(): message = lax.ppermute(message, 'ascan', pairs)  14.7 us
    pallas_call x4, Pallas kernels, send(): pl.pallas_call(functools.partial(send_kernel, peers, messages), out_shape...  13.7 us
    ppermute x3, starting transfers between devices, sparse_body(): shares.append(lax.ppermute(stats, 'ascan', flipped(members, bits)))  12.1 us
    ppermute x3, waiting for transfers between devices, sparse_body(): shares.append(lax.ppermute(stats, 'ascan', flipped(members, bits)))  8.74 us
    ppermute x3, waiting for transfers between devices, sparse_body(): stats = stats + lax.ppermute(stats, axis, pairs)  6.85 us
    pallas_call x1, Pallas kernels, result_call(): pl.pallas_call(kernel, out_shape=[shape] * MAPS + list(extra), in_specs=[...  4.36 us
  transfers between devices with their start and end apart: 21, of which 11 were waited for; matrix products, arithmetic and copies ran while one was open for 0% of the time, Pallas kernels for 12%

profile of v2, /device:TPU:2, one launch (start us, length us, event | category | flops | bytes accessed | tf_op | source)
XLA Modules:
  0.0 91.2 jit_solution(11014888629652021459)
XLA Ops:
  0.6 0.0 copy-start
  0.7 0.0 copy-start.2
  0.7 0.0 copy-start.3
  0.7 0.0 copy-start.4
  0.7 3.6 %shard_map.84 = (f32[96,384]{1,0:T(8,128)S(1)}, f32[56,384]{1,0:T(8,128)S(1)}, f32[72,384]{1,0:T(8,128)S(1)}, f32[8,128]{1,0:T(8,128)S(1)}) custom-call(bf16[2,4,128,2048]{3,2,1,0:T(8,128)(2,1)} %x_ref.7, bf16[8,512,256]{2,1,0:T(8,128)(2,1)} %constant.14.table_ref, s32[2,128]{1,0:T(2,128)} %top_ref.11, s32[2,128]{1,0:T(2,128)} %bottom_ref.11, ...), custom_call_target="tpu_custom_call" | custom-call | flops 1073741824 | bytes 4194304 | tf_op jit(solution)/shard_map/pallas_call | solution.py:286
  4.3 1.4 %collective-permute-start.7 = (f32[56,384]{1,0:T(8,128)S(1)}, f32[56,384]{1,0:T(8,128)S(1)}, u32[]{:S(2)}, u32[]{:S(2)}) collective-permute-start(f32[56,384]{1,0:T(8,128)S(1)} %get-tuple-element.88), channel_id=1, source_target_pairs={{5,1},{6,2},{7,3},{13,9},{14,10},{15,11},{21,17},{22,18},{23,19},{... | collective-permute-start | bytes 258056 | tf_op jit(solution)/shard_map/ppermute | solution.py:550
  5.7 0.0 copy-done
  5.7 0.0 copy-done.2
  5.7 0.0 copy-done.3
  5.7 0.0 copy-done.4
  5.7 0.6 shard_map.85
  6.4 1.3 %collective-permute-start.9 = (f32[56,384]{1,0:T(8,128)S(1)}, f32[56,384]{1,0:T(8,128)S(1)}, u32[]{:S(2)}, u32[]{:S(2)}) collective-permute-start(f32[56,384]{1,0:T(8,128)S(1)} %get-tuple-element.90), channel_id=1, source_target_pairs={{4,1},{5,2},{6,3},{12,9},{13,10},{14,11},{20,17},{21,18},{22,19},{... | collective-permute-start | bytes 258056 | tf_op jit(solution)/shard_map/ppermute | solution.py:550
  7.7 1.0 %shard_map.86 = (f32[96,384]{1,0:T(8,128)S(1)}, f32[56,384]{1,0:T(8,128)S(1)}, f32[56,384]{1,0:T(8,128)S(1)}, f32[96,384]{1,0:T(8,128)S(1)}, f32[56,384]{1,0:T(8...) custom-call(bf16[2,4,128,2048]{3,2,1,0:T(8,128)(2,1)S(1)} %copy-done, bf16[8,512,256]{2,1,0:T(8,128)(2,1)S(1)} %copy-done.2, ...), custom_call_target="tpu_custom_call" | custom-call | flops 2147483648 | bytes 4194304 | tf_op jit(solution)/shard_map/pallas_call | solution.py:286
  8.6 0.7 collective-permute-start.14
  9.3 0.0 copy-start.5
  9.3 8.5 %shard_map.87 = (f32[184,384]{1,0:T(8,128)S(1)}, f32[184,384]{1,0:T(8,128)S(1)}, f32[184,384]{1,0:T(8,128)S(1)}, f32[256,384]{1,0:T(8,128)S(1)}, f32[8,128]{1,0:T(8,128)S(1)}) custom-call(bf16[2,4,128,2048]{3,2,1,0:T(8,128)(2,1)S(1)} %copy-done, bf16[8,512,256]{2,1,0:T(8,128)(2,1)S(1)} %copy-done.2, s32[2,128]{1,0:T(2,128)S(1)} %copy-done.3, ...), custom_call_target="tpu_custom_call" | custom-call | flops 4294967296 | bytes 4194304 | tf_op jit(solution)/shard_map/pallas_call | solution.py:286
  17.9 0.1 collective-permute-start.15
  18.0 3.6 %collective-permute-done.15 = f32[8,128]{1,0:T(8,128)S(1)} collective-permute-done((f32[8,128]{1,0:T(8,128)S(1)}, f32[8,128]{1,0:T(8,128)S(1)}, u32[]{:S(2)}, u32[]{:S(2)}) %collective-permute-start.15) | collective-permute-done | bytes 4128 | tf_op jit(solution)/shard_map/ppermute | solution.py:544
  21.5 0.0 collective-permute-start.16
  21.6 1.2 %collective-permute-done.16 = f32[8,128]{1,0:T(8,128)S(1)} collective-permute-done((f32[8,128]{1,0:T(8,128)S(1)}, f32[8,128]{1,0:T(8,128)S(1)}, u32[]{:S(2)}, u32[]{:S(2)}) %collective-permute-start.16) | collective-permute-done | bytes 4128 | tf_op jit(solution)/shard_map/ppermute | solution.py:544
  22.7 1.5 %collective-permute-start.17 = (f32[8,128]{1,0:T(8,128)S(1)}, f32[8,128]{1,0:T(8,128)S(1)}, u32[]{:S(2)}, u32[]{:S(2)}) collective-permute-start(f32[8,128]{1,0:T(8,128)S(1)} %add.10), channel_id=1, source_target_pairs={{0,16},{8,24},{16,0},{24,8},{1,17},{9,25},{17,1},{25,9},{2,18},{10... | collective-permute-start | bytes 12296 | tf_op jit(solution)/shard_map/ppermute | solution.py:544
  24.2 2.1 %collective-permute-done.17 = f32[8,128]{1,0:T(8,128)S(1)} collective-permute-done((f32[8,128]{1,0:T(8,128)S(1)}, f32[8,128]{1,0:T(8,128)S(1)}, u32[]{:S(2)}, u32[]{:S(2)}) %collective-permute-start.17) | collective-permute-done | bytes 4128 | tf_op jit(solution)/shard_map/ppermute | solution.py:544
  26.3 9.4 %collective-permute-start.20 = (f32[8,128]{1,0:T(8,128)S(1)}, f32[8,128]{1,0:T(8,128)S(1)}, u32[]{:S(2)}, u32[]{:S(2)}) collective-permute-start(f32[8,128]{1,0:T(8,128)S(1)} %add.11), channel_id=1, source_target_pairs={{0,6},{1,7},{2,4},{3,5},{4,2},{5,3},{6,0},{7,1},{8,14},{9,15},{10,... | collective-permute-start | bytes 12296 | tf_op jit(solution)/shard_map/ppermute | solution.py:553
  35.8 0.0 collective-permute-start
  35.8 1.6 %collective-permute-done.20 = f32[8,128]{1,0:T(8,128)S(1)} collective-permute-done((f32[8,128]{1,0:T(8,128)S(1)}, f32[8,128]{1,0:T(8,128)S(1)}, u32[]{:S(2)}, u32[]{:S(2)}) %collective-permute-start.20) | collective-permute-done | bytes 4128 | tf_op jit(solution)/shard_map/ppermute | solution.py:553
  37.4 2.6 %collective-permute-start.19 = (f32[8,128]{1,0:T(8,128)S(1)}, f32[8,128]{1,0:T(8,128)S(1)}, u32[]{:S(2)}, u32[]{:S(2)}) collective-permute-start(f32[8,128]{1,0:T(8,128)S(1)} %add.11), channel_id=1, source_target_pairs={{0,4},{1,5},{2,6},{3,7},{4,0},{5,1},{6,2},{7,3},{8,12},{9,13},{10,... | collective-permute-start | bytes 12296 | tf_op jit(solution)/shard_map/ppermute | solution.py:553
  40.0 3.5 %collective-permute-done.19 = f32[8,128]{1,0:T(8,128)S(1)} collective-permute-done((f32[8,128]{1,0:T(8,128)S(1)}, f32[8,128]{1,0:T(8,128)S(1)}, u32[]{:S(2)}, u32[]{:S(2)}) %collective-permute-start.19) | collective-permute-done | bytes 4128 | tf_op jit(solution)/shard_map/ppermute | solution.py:553
  43.5 0.0 collective-permute-start.18
  43.5 3.6 %collective-permute-done.18 = f32[8,128]{1,0:T(8,128)S(1)} collective-permute-done((f32[8,128]{1,0:T(8,128)S(1)}, f32[8,128]{1,0:T(8,128)S(1)}, u32[]{:S(2)}, u32[]{:S(2)}) %collective-permute-start.18) | collective-permute-done | bytes 4128 | tf_op jit(solution)/shard_map/ppermute | solution.py:553
  47.1 2.2 %collective-permute-start.1 = (f32[96,384]{1,0:T(8,128)S(1)}, f32[96,384]{1,0:T(8,128)S(1)}, u32[]{:S(2)}, u32[]{:S(2)}) collective-permute-start(f32[96,384]{1,0:T(8,128)S(1)} %get-tuple-element.80), channel_id=1, source_target_pairs={{0,5},{1,6},{2,7},{3,4},{4,1},{5,2},{6,3},{7,0},{8,13},{9,14},{10,... | collective-permute-start | bytes 442376 | tf_op jit(solution)/shard_map/ppermute | solution.py:550
  49.4 0.0 collective-permute-done.14.refs_11_
  49.4 0.2 collective-permute-start.4
  49.6 0.0 collective-permute-done.7.refs_1_
  49.6 1.7 %collective-permute-start.5 = (f32[184,384]{1,0:T(8,128)S(1)}, f32[184,384]{1,0:T(8,128)S(1)}, u32[]{:S(2)}, u32[]{:S(2)}) collective-permute-start(f32[184,384]{1,0:T(8,128)S(1)} %get-tuple-element.86), channel_id=1, source_target_pairs={{0,2},{1,3},{2,0},{3,1},{4,6},{5,7},{6,4},{7,5},{8,10},{9,11},{10,... | collective-permute-start | bytes 847880 | tf_op jit(solution)/shard_map/ppermute | solution.py:550
  51.3 0.0 collective-permute-done.9.refs_4_
  51.3 1.6 %collective-permute-start.6 = (f32[184,384]{1,0:T(8,128)S(1)}, f32[184,384]{1,0:T(8,128)S(1)}, u32[]{:S(2)}, u32[]{:S(2)}) collective-permute-start(f32[184,384]{1,0:T(8,128)S(1)} %get-tuple-element.87), channel_id=1, source_target_pairs={{0,3},{1,2},{2,1},{3,0},{4,7},{5,6},{6,5},{7,4},{8,11},{9,10},{10,... | collective-permute-start | bytes 847880 | tf_op jit(solution)/shard_map/ppermute | solution.py:550
  52.9 0.0 collective-permute-done.refs_0_
  52.9 1.1 %collective-permute-start.2 = (f32[96,384]{1,0:T(8,128)S(1)}, f32[96,384]{1,0:T(8,128)S(1)}, u32[]{:S(2)}, u32[]{:S(2)}) collective-permute-start(f32[96,384]{1,0:T(8,128)S(1)} %get-tuple-element.82), channel_id=1, source_target_pairs={{0,6},{1,7},{2,4},{3,5},{4,2},{5,3},{6,0},{7,1},{8,14},{9,15},{10,... | collective-permute-start | bytes 442376 | tf_op jit(solution)/shard_map/ppermute | solution.py:550
  53.9 3.0 %collective-permute-done.1.refs_1_.refs_3_ = f32[96,384]{1,0:T(8,128)S(1)} collective-permute-done((f32[96,384]{1,0:T(8,128)S(1)}, f32[96,384]{1,0:T(8,128)S(1)}, u32[]{:S(2)}, u32[]{:S(2)}) %collective-permute-start.1) | collective-permute-done | bytes 147488 | tf_op jit(solution)/shard_map/ppermute | solution.py:550
  57.0 0.0 collective-permute-start.3
  57.0 13.4 %collective-permute-done.2.refs_2_.refs_6_ = f32[96,384]{1,0:T(8,128)S(1)} collective-permute-done((f32[96,384]{1,0:T(8,128)S(1)}, f32[96,384]{1,0:T(8,128)S(1)}, u32[]{:S(2)}, u32[]{:S(2)}) %collective-permute-start.2) | collective-permute-done | bytes 147488 | tf_op jit(solution)/shard_map/ppermute | solution.py:550
  70.4 0.7 collective-permute-start.8
  71.1 2.3 %collective-permute-done.3.refs_3_.refs_9_ = f32[96,384]{1,0:T(8,128)S(1)} collective-permute-done((f32[96,384]{1,0:T(8,128)S(1)}, f32[96,384]{1,0:T(8,128)S(1)}, u32[]{:S(2)}, u32[]{:S(2)}) %collective-permute-start.3) | collective-permute-done | bytes 147488 | tf_op jit(solution)/shard_map/ppermute | solution.py:550
  73.4 0.7 collective-permute-start.10
  74.1 0.0 collective-permute-done.4.refs_4_.refs_12_
  74.1 1.3 %collective-permute-start.11 = (f32[56,384]{1,0:T(8,128)S(1)}, f32[56,384]{1,0:T(8,128)S(1)}, u32[]{:S(2)}, u32[]{:S(2)}) collective-permute-start(f32[56,384]{1,0:T(8,128)S(1)} %get-tuple-element.92), channel_id=1, source_target_pairs={{4,2},{5,3},{7,1},{12,10},{13,11},{15,9},{20,18},{21,19},{23,17},{... | collective-permute-start | bytes 258056 | tf_op jit(solution)/shard_map/ppermute | solution.py:550
  75.4 0.0 collective-permute-done.5.refs_5_.refs_13_
  75.4 0.7 collective-permute-start.12
  76.1 0.0 collective-permute-done.6.refs_6_.refs_14_
  76.1 1.3 %collective-permute-start.13 = (f32[56,384]{1,0:T(8,128)S(1)}, f32[56,384]{1,0:T(8,128)S(1)}, u32[]{:S(2)}, u32[]{:S(2)}) collective-permute-start(f32[56,384]{1,0:T(8,128)S(1)} %get-tuple-element.94), channel_id=1, source_target_pairs={{4,3},{6,1},{7,2},{12,11},{14,9},{15,10},{20,19},{22,17},{23,18},{... | collective-permute-start | bytes 258056 | tf_op jit(solution)/shard_map/ppermute | solution.py:550
  77.4 0.0 copy-done.5
  77.4 0.1 jit_solution_.3.room_ref
  77.4 0.7 judge_room.1
  78.8 3.5 %collective-permute-done.11.refs_7_ = f32[56,384]{1,0:T(8,128)S(1)} collective-permute-done((f32[56,384]{1,0:T(8,128)S(1)}, f32[56,384]{1,0:T(8,128)S(1)}, u32[]{:S(2)}, u32[]{:S(2)}) %collective-permute-start.11) | collective-permute-done | bytes 86048 | tf_op jit(solution)/shard_map/ppermute | solution.py:550
  82.4 0.0 collective-permute-done.12.refs_8_
  82.4 2.8 %collective-permute-done.13.refs_10_ = f32[56,384]{1,0:T(8,128)S(1)} collective-permute-done((f32[56,384]{1,0:T(8,128)S(1)}, f32[56,384]{1,0:T(8,128)S(1)}, u32[]{:S(2)}, u32[]{:S(2)}) %collective-permute-start.13) | collective-permute-done | bytes 86048 | tf_op jit(solution)/shard_map/ppermute | solution.py:550
  85.1 0.0 collective-permute-done.10.refs_5_
  85.1 0.0 collective-permute-done.8.refs_2_
  85.1 4.4 %shard_map.88 = (f32[2,128,1024]{2,1,0:T(8,128)S(1)}, f32[2,128,1024]{2,1,0:T(8,128)}, f32[2,128,1024]{2,1,0:T(8,128)}) custom-call(s32[2,128]{1,0:T(2,128)S(1)} %copy-done.3, s32[2,128]{1,0:T(2,128)S(1)} %copy-done.4, f32[96,384]{1,0:T(8,128)S(1)} %collective-permute-done.refs_0_, f32[56,384]{1,0:T(8,128)S(1)} %collective-permute-done.7.refs_1_, ...), custom_call_target="tpu_custom_call" | custom-call | flops 805306368 | bytes 6291456 | tf_op jit(solution)/shard_map/pallas_call | solution.py:449
  89.5 1.2 %conditional.1 = ((f32[2,128,1024]{2,1,0:T(8,128)}, f32[2,128,1024]{2,1,0:T(8,128)}, f32[2,128,1024]{2,1,0:T(8,128)}, f32[8,128]{1,0:T(8,128)S(1)})) conditional(s32[]{:T(128)} %bitcast, (f32[2,128,1024]{2,1,0:T(8,128)S(1)}, f32[8,128]{1,0:T(8,128)S(1)}, f32[8,128]{1,0:T(8,128)S(1)}, f32[8,128]{1,0:T(8,128)S(1)}, f32[8,128]{1,0:T(8,128)S(1)}, ...), branch_computations={%region_0.0_spmd, %region_1.0_spmd} | conditional | flops 805306368 | bytes 29360164 | solution.py:587
  89.5 1.2 %finish_angiogram.1 = (f32[2,128,1024]{2,1,0:T(8,128)}, f32[8,128]{1,0:T(8,128)S(1)}) custom-call(f32[2,128,1024]{2,1,0:T(8,128)S(1)} %get-tuple-element.30.sums_ref, f32[8,128]{1,0:T(8,128)S(1)} %get-tuple-element.31.refs_0_, f32[8,128]{1,0:T(8,128)S(1)} %get-tuple-element.32.refs_1_, f32[8,128]{1,0:T(8,128)S(1)} %get-tuple-element.33.refs_2_, ...), custom_call_target="tpu_custom_call" | custom-call | tf_op jit(solution)/shard_map/cond/branch_0_fun/finish_angiogram/pallas_call | solution.py:376
  90.7 0.5 slice.3
  (4 shorter events, 0.0 us)
Async XLA Ops:
  0.6 5.1 %copy-start = (bf16[2,4,128,2048]{3,2,1,0:T(8,128)(2,1)S(1)}, bf16[2,4,128,2048]{3,2,1,0:T(8,128)(2,1)}, u32[]{:S(2)}) copy-start(bf16[2,4,128,2048]{3,2,1,0:T(8,128)(2,1)} %x_ref.7) | copy-start | bytes 12582916
  0.7 5.1 %copy-start.2 = (bf16[8,512,256]{2,1,0:T(8,128)(2,1)S(1)}, bf16[8,512,256]{2,1,0:T(8,128)(2,1)}, u32[]{:S(2)}) copy-start(bf16[8,512,256]{2,1,0:T(8,128)(2,1)} %constant.14.table_ref) | copy-start | bytes 6291460
  0.7 5.1 %copy-start.3 = (s32[2,128]{1,0:T(2,128)S(1)}, s32[2,128]{1,0:T(2,128)}, u32[]{:S(2)}) copy-start(s32[2,128]{1,0:T(2,128)} %top_ref.11) | copy-start | bytes 3076
  0.7 5.1 %copy-start.4 = (s32[2,128]{1,0:T(2,128)S(1)}, s32[2,128]{1,0:T(2,128)}, u32[]{:S(2)}) copy-start(s32[2,128]{1,0:T(2,128)} %bottom_ref.11) | copy-start | bytes 3076
  4.3 45.3 %collective-permute-start.7 = (f32[56,384]{1,0:T(8,128)S(1)}, f32[56,384]{1,0:T(8,128)S(1)}, u32[]{:S(2)}, u32[]{:S(2)}) collective-permute-start(f32[56,384]{1,0:T(8,128)S(1)} %get-tuple-element.88), channel_id=1, source_target_pairs={{5,1},{6,2},{7,3},{13,9},{14,10},{15,11},{21,17},{22,18},{23,19},{... | collective-permute-start | bytes 258056 | tf_op jit(solution)/shard_map/ppermute | solution.py:550
  6.4 44.9 %collective-permute-start.9 = (f32[56,384]{1,0:T(8,128)S(1)}, f32[56,384]{1,0:T(8,128)S(1)}, u32[]{:S(2)}, u32[]{:S(2)}) collective-permute-start(f32[56,384]{1,0:T(8,128)S(1)} %get-tuple-element.90), channel_id=1, source_target_pairs={{4,1},{5,2},{6,3},{12,9},{13,10},{14,11},{20,17},{21,18},{22,19},{... | collective-permute-start | bytes 258056 | tf_op jit(solution)/shard_map/ppermute | solution.py:550
  8.6 40.7 %collective-permute-start.14 = (f32[48,384]{1,0:T(8,128)S(1)}, f32[48,384]{1,0:T(8,128)S(1)}, u32[]{:S(2)}, u32[]{:S(2)}) collective-permute-start(f32[48,384]{1,0:T(8,128)S(1)} %get-tuple-element.95), channel_id=1, source_target_pairs={{4,3},{7,2},{12,11},{15,10},{20,19},{23,18},{28,27},{31,26}} | collective-permute-start | bytes 221192 | tf_op jit(solution)/shard_map/ppermute | solution.py:550
  9.3 68.0 %copy-start.5 = (f32[8,8]{1,0:T(8,128)S(1)}, f32[8,8]{1,0:T(8,128)}, u32[]{:S(2)}) copy-start(f32[8,8]{1,0:T(8,128)} %constant.10.clone) | copy-start | bytes 772
  17.9 3.7 %collective-permute-start.15 = (f32[8,128]{1,0:T(8,128)S(1)}, f32[8,128]{1,0:T(8,128)S(1)}, u32[]{:S(2)}, u32[]{:S(2)}) collective-permute-start(f32[8,128]{1,0:T(8,128)S(1)} %get-tuple-element.98), channel_id=1, source_target_pairs={{0,1},{1,0},{2,3},{3,2},{4,5},{5,4},{6,7},{7,6},{8,9},{9,8},{10,11... | collective-permute-start | bytes 12296 | tf_op jit(solution)/shard_map/ppermute | solution.py:544
  21.5 1.2 %collective-permute-start.16 = (f32[8,128]{1,0:T(8,128)S(1)}, f32[8,128]{1,0:T(8,128)S(1)}, u32[]{:S(2)}, u32[]{:S(2)}) collective-permute-start(f32[8,128]{1,0:T(8,128)S(1)} %add.9), channel_id=1, source_target_pairs={{0,8},{8,0},{16,24},{24,16},{1,9},{9,1},{17,25},{25,17},{2,10},{10... | collective-permute-start | bytes 12296 | tf_op jit(solution)/shard_map/ppermute | solution.py:544
  22.7 3.6 %collective-permute-start.17 = (f32[8,128]{1,0:T(8,128)S(1)}, f32[8,128]{1,0:T(8,128)S(1)}, u32[]{:S(2)}, u32[]{:S(2)}) collective-permute-start(f32[8,128]{1,0:T(8,128)S(1)} %add.10), channel_id=1, source_target_pairs={{0,16},{8,24},{16,0},{24,8},{1,17},{9,25},{17,1},{25,9},{2,18},{10... | collective-permute-start | bytes 12296 | tf_op jit(solution)/shard_map/ppermute | solution.py:544
  26.3 11.1 %collective-permute-start.20 = (f32[8,128]{1,0:T(8,128)S(1)}, f32[8,128]{1,0:T(8,128)S(1)}, u32[]{:S(2)}, u32[]{:S(2)}) collective-permute-start(f32[8,128]{1,0:T(8,128)S(1)} %add.11), channel_id=1, source_target_pairs={{0,6},{1,7},{2,4},{3,5},{4,2},{5,3},{6,0},{7,1},{8,14},{9,15},{10,... | collective-permute-start | bytes 12296 | tf_op jit(solution)/shard_map/ppermute | solution.py:553
  35.8 17.1 %collective-permute-start = (f32[96,384]{1,0:T(8,128)S(1)}, f32[96,384]{1,0:T(8,128)S(1)}, u32[]{:S(2)}, u32[]{:S(2)}) collective-permute-start(f32[96,384]{1,0:T(8,128)S(1)} %get-tuple-element.78), channel_id=1, source_target_pairs={{0,4},{1,5},{2,6},{3,7},{4,0},{5,1},{6,2},{7,3},{8,12},{9,13},{10,... | collective-permute-start | bytes 442376 | tf_op jit(solution)/shard_map/ppermute | solution.py:550
  37.4 6.1 %collective-permute-start.19 = (f32[8,128]{1,0:T(8,128)S(1)}, f32[8,128]{1,0:T(8,128)S(1)}, u32[]{:S(2)}, u32[]{:S(2)}) collective-permute-start(f32[8,128]{1,0:T(8,128)S(1)} %add.11), channel_id=1, source_target_pairs={{0,4},{1,5},{2,6},{3,7},{4,0},{5,1},{6,2},{7,3},{8,12},{9,13},{10,... | collective-permute-start | bytes 12296 | tf_op jit(solution)/shard_map/ppermute | solution.py:553
  43.5 3.6 %collective-permute-start.18 = (f32[8,128]{1,0:T(8,128)S(1)}, f32[8,128]{1,0:T(8,128)S(1)}, u32[]{:S(2)}, u32[]{:S(2)}) collective-permute-start(f32[8,128]{1,0:T(8,128)S(1)} %add.11), channel_id=1, source_target_pairs={{0,2},{1,3},{2,0},{3,1},{4,6},{5,7},{6,4},{7,5},{8,10},{9,11},{10,... | collective-permute-start | bytes 12296 | tf_op jit(solution)/shard_map/ppermute | solution.py:553
  47.1 9.8 %collective-permute-start.1 = (f32[96,384]{1,0:T(8,128)S(1)}, f32[96,384]{1,0:T(8,128)S(1)}, u32[]{:S(2)}, u32[]{:S(2)}) collective-permute-start(f32[96,384]{1,0:T(8,128)S(1)} %get-tuple-element.80), channel_id=1, source_target_pairs={{0,5},{1,6},{2,7},{3,4},{4,1},{5,2},{6,3},{7,0},{8,13},{9,14},{10,... | collective-permute-start | bytes 442376 | tf_op jit(solution)/shard_map/ppermute | solution.py:550
  49.4 24.7 %collective-permute-start.4 = (f32[184,384]{1,0:T(8,128)S(1)}, f32[184,384]{1,0:T(8,128)S(1)}, u32[]{:S(2)}, u32[]{:S(2)}) collective-permute-start(f32[184,384]{1,0:T(8,128)S(1)} %get-tuple-element.85), channel_id=1, source_target_pairs={{0,1},{1,0},{2,3},{3,2},{4,5},{5,4},{6,7},{7,6},{8,9},{9,8},{10,11... | collective-permute-start | bytes 847880 | tf_op jit(solution)/shard_map/ppermute | solution.py:550
  49.6 25.8 %collective-permute-start.5 = (f32[184,384]{1,0:T(8,128)S(1)}, f32[184,384]{1,0:T(8,128)S(1)}, u32[]{:S(2)}, u32[]{:S(2)}) collective-permute-start(f32[184,384]{1,0:T(8,128)S(1)} %get-tuple-element.86), channel_id=1, source_target_pairs={{0,2},{1,3},{2,0},{3,1},{4,6},{5,7},{6,4},{7,5},{8,10},{9,11},{10,... | collective-permute-start | bytes 847880 | tf_op jit(solution)/shard_map/ppermute | solution.py:550
  51.3 24.7 %collective-permute-start.6 = (f32[184,384]{1,0:T(8,128)S(1)}, f32[184,384]{1,0:T(8,128)S(1)}, u32[]{:S(2)}, u32[]{:S(2)}) collective-permute-start(f32[184,384]{1,0:T(8,128)S(1)} %get-tuple-element.87), channel_id=1, source_target_pairs={{0,3},{1,2},{2,1},{3,0},{4,7},{5,6},{6,5},{7,4},{8,11},{9,10},{10,... | collective-permute-start | bytes 847880 | tf_op jit(solution)/shard_map/ppermute | solution.py:550
  52.9 17.5 %collective-permute-start.2 = (f32[96,384]{1,0:T(8,128)S(1)}, f32[96,384]{1,0:T(8,128)S(1)}, u32[]{:S(2)}, u32[]{:S(2)}) collective-permute-start(f32[96,384]{1,0:T(8,128)S(1)} %get-tuple-element.82), channel_id=1, source_target_pairs={{0,6},{1,7},{2,4},{3,5},{4,2},{5,3},{6,0},{7,1},{8,14},{9,15},{10,... | collective-permute-start | bytes 442376 | tf_op jit(solution)/shard_map/ppermute | solution.py:550
  57.0 16.4 %collective-permute-start.3 = (f32[96,384]{1,0:T(8,128)S(1)}, f32[96,384]{1,0:T(8,128)S(1)}, u32[]{:S(2)}, u32[]{:S(2)}) collective-permute-start(f32[96,384]{1,0:T(8,128)S(1)} %get-tuple-element.83), channel_id=1, source_target_pairs={{0,7},{1,4},{2,5},{3,6},{4,3},{5,0},{6,1},{7,2},{8,15},{9,12},{10,... | collective-permute-start | bytes 442376 | tf_op jit(solution)/shard_map/ppermute | solution.py:550
  70.4 14.7 %collective-permute-start.8 = (f32[72,384]{1,0:T(8,128)S(1)}, f32[72,384]{1,0:T(8,128)S(1)}, u32[]{:S(2)}, u32[]{:S(2)}) collective-permute-start(f32[72,384]{1,0:T(8,128)S(1)} %get-tuple-element.89), channel_id=1, source_target_pairs={{6,2},{7,3},{14,10},{15,11},{22,18},{23,19},{30,26},{31,27}} | collective-permute-start | bytes 331784 | tf_op jit(solution)/shard_map/ppermute | solution.py:550
  73.4 11.7 %collective-permute-start.10 = (f32[64,384]{1,0:T(8,128)S(1)}, f32[64,384]{1,0:T(8,128)S(1)}, u32[]{:S(2)}, u32[]{:S(2)}) collective-permute-start(f32[64,384]{1,0:T(8,128)S(1)} %get-tuple-element.91), channel_id=1, source_target_pairs={{5,2},{6,3},{13,10},{14,11},{21,18},{22,19},{29,26},{30,27}} | collective-permute-start | bytes 294920 | tf_op jit(solution)/shard_map/ppermute | solution.py:550
  74.1 8.3 %collective-permute-start.11 = (f32[56,384]{1,0:T(8,128)S(1)}, f32[56,384]{1,0:T(8,128)S(1)}, u32[]{:S(2)}, u32[]{:S(2)}) collective-permute-start(f32[56,384]{1,0:T(8,128)S(1)} %get-tuple-element.92), channel_id=1, source_target_pairs={{4,2},{5,3},{7,1},{12,10},{13,11},{15,9},{20,18},{21,19},{23,17},{... | collective-permute-start | bytes 258056 | tf_op jit(solution)/shard_map/ppermute | solution.py:550
  75.4 7.0 %collective-permute-start.12 = (f32[56,384]{1,0:T(8,128)S(1)}, f32[56,384]{1,0:T(8,128)S(1)}, u32[]{:S(2)}, u32[]{:S(2)}) collective-permute-start(f32[56,384]{1,0:T(8,128)S(1)} %get-tuple-element.93), channel_id=1, source_target_pairs={{4,2},{5,3},{12,10},{13,11},{20,18},{21,19},{28,26},{29,27}} | collective-permute-start | bytes 258056 | tf_op jit(solution)/shard_map/ppermute | solution.py:550
  76.1 9.1 %collective-permute-start.13 = (f32[56,384]{1,0:T(8,128)S(1)}, f32[56,384]{1,0:T(8,128)S(1)}, u32[]{:S(2)}, u32[]{:S(2)}) collective-permute-start(f32[56,384]{1,0:T(8,128)S(1)} %get-tuple-element.94), channel_id=1, source_target_pairs={{4,3},{6,1},{7,2},{12,11},{14,9},{15,10},{20,19},{22,17},{23,18},{... | collective-permute-start | bytes 258056 | tf_op jit(solution)/shard_map/ppermute | solution.py:550
